TPU v7x, 32 devices: a whole 2x2x4 slice. The times are simulated.
32 devices in a mesh: group: 2 (over core), gx: 4 (over y, x), gy: 4 (over z).
Axes of the slice: x: 2, y: 2, z: 4, core: 2. Of those that a mesh axis runs over, the one named last changes fastest.
Arguments:
- forcing: float32 [2, 80, 32, 1024], P('group', None, 'gx', 'gy'), may hold values from -24 to 24
- conduct: bfloat16 [2, 80, 32, 1024], P('group', None, 'gx', 'gy'), may hold values from 0.25 to 4
- diag_add: bfloat16 [2, 80, 32, 1024], P('group', None, 'gx', 'gy'), may hold values from 0.049804688 to 0.5
- ice_mask: int32 [32, 1024], P('gx', 'gy'), may hold values 0 or 1
- grounded: int32 [32, 1024], P('gx', 'gy'), may hold values 0 or 1
Outputs:
- solution: float32 [2, 80, 32, 1024], P('group', None, 'gx', 'gy')
- residual: float32 [2, 80, 32, 1024], P('group', None, 'gx', 'gy')
All inputs are finite; a program needn't handle non-finite values. No bound on the sum of `ice_mask` or of `grounded` on one device may be relied on, other than what follows from the above.
Results may differ from a plain program's by a relative error of at most 0.0003.
Values sent between devices are 32-bit elements; how exact they have to be, the bound alone decides.
A program may use at most 64 MiB of HBM per device.

v0:
```python
import functools

import jax
import jax.numpy as jnp
from jax import lax
from jax.experimental import pallas as pl
from jax.experimental.pallas import tpu as pltpu
from jax.sharding import PartitionSpec as P

ITERS = 6
far_weight = 0.25
cross_weight = 0.5
vertical_weight = 4.0
friction_gain = 8.0
SUB = 8
LANES = 128
CHUNK_TILES = (1,)


def coefficients(moments):
    def gram(j, k):
        return 0.5 * (moments[j + k] + moments[abs(j - k)])

    table = {(j, k): gram(j, k) for j in range(ITERS + 1) for k in range(j, ITERS + 1)}

    def form(a, b):
        terms = []
        for j in range(len(a)):
            row = None
            for k in range(len(b)):
                term = table[min(j, k), max(j, k)] * b[k]
                row = term if row is None else row + term
            terms.append(a[j] * row)
        return functools.reduce(lambda s, t: s + t, terms)

    def shift(e):
        out = [jnp.zeros_like(e[0]) for _ in range(len(e) + 1)]
        for k, value in enumerate(e):
            if k == 0:
                out[1] = out[1] + value
            else:
                out[k + 1] = out[k + 1] + 0.5 * value
                out[k - 1] = out[k - 1] + 0.5 * value
        return out

    left = [jnp.ones_like(moments[0])]
    direction = list(left)
    iterate = []
    norm_now = form(left, left)
    for iteration in range(ITERS):
        moved = shift(direction)
        applied = [
            (direction[k] - moved[k]) if k < len(direction) else -moved[k]
            for k in range(len(moved))
        ]
        step = norm_now / form(direction, applied)
        iterate = [
            (iterate[k] if k < len(iterate) else 0.0) + step * direction[k]
            for k in range(len(direction))
        ]
        left = [
            (left[k] - step * applied[k]) if k < len(left) else -step * applied[k]
            for k in range(len(applied))
        ]
        if iteration + 1 < ITERS:
            norm_next = form(left, left)
            ratio = norm_next / norm_now
            direction = [
                left[k] + (ratio * direction[k] if k < len(direction) else 0.0)
                for k in range(len(left))
            ]
            norm_now = norm_next
    return iterate, left


def kernel(
    sizes,
    force,
    conduct,
    extra,
    ice,
    grounded,
    out_x,
    out_r,
    field,
    pack,
    rim_right,
    rim_left,
    corner,
    cornered,
    held,
    basis,
    coupling,
    scaled,
    diagonal,
    share,
    shared,
    partial,
    sum_x,
    sum_y,
    send_sem,
    recv_sem,
    share_sem,
    detour_sem,
    sx_send,
    sx_recv,
    sy_send,
    sy_recv,
):
    nx, ny = sizes
    rows, layers, width = force.shape
    tiles = layers // SUB
    chunks = corner.shape[1]
    per = tiles // chunks
    deep = per * SUB
    gg, gx, gy = lax.axis_index("group"), lax.axis_index("gx"), lax.axis_index("gy")
    is_ice = gg == 0

    def there(dx, dy):
        ok = None
        for d, g, n in ((dx, gx, nx), (dy, gy, ny)):
            if d != 0:
                one = (g + d >= 0) & (g + d < n)
                ok = one if ok is None else ok & one
        return ok

    def at(dx, dy):
        return (gg, gx + dx, gy + dy)

    two = 2 * rows
    sides = ((-1, 0), (1, 0), (0, -1), (0, 1), (-1, -1), (1, -1), (-1, 1), (1, 1))

    def copy_of(i, p, c, span=2):
        dx, dy = sides[i]
        inner = pl.ds(pl.multiple_of(c * deep + SUB, SUB), deep)
        flat = pl.ds(pl.multiple_of(c * deep, SUB), deep)
        if i == 0:
            source = field.at[p, 2 : 2 + span, inner]
            target = field.at[p, rows + 2 : rows + 2 + span, inner]
        elif i == 1:
            source = field.at[p, rows : rows + span, inner]
            target = field.at[p, 0:span, inner]
        elif i == 2:
            source, target = pack.at[p, flat], rim_right.at[p, flat]
        elif i == 3:
            source, target = pack.at[p, flat], rim_left.at[p, flat]
        else:
            source, target = corner.at[p, c], cornered.at[p, c, i - 4]
        return pltpu.make_async_remote_copy(
            src_ref=source,
            dst_ref=target,
            send_sem=send_sem.at[p, c, i],
            recv_sem=recv_sem.at[p, c, i],
            device_id=at(dx, dy),
            device_id_type=pl.DeviceIdType.MESH,
        )

    detours = ((1, 3, 2, rows + 1, 1), (2, 0, 1, 3, rows + 3)) if nx == 4 else ()
    lag = min(4, chunks - 1)

    def each(toward, act):
        for i, (dx, dy) in enumerate(sides):
            ok = there(toward * dx, toward * dy)
            if i < 2 and detours:
                split = gx == ((2 - i) if toward > 0 else (1 + i))

                @pl.when(split)
                def _():
                    act(i, 1)

                ok = ok & jnp.logical_not(split)

            @pl.when(ok)
            def _():
                act(i, 2)

    def away(path, p, c, slot):
        origin, relay, _, row, _ = path
        return pltpu.make_async_remote_copy(
            src_ref=field.at[p, row, pl.ds(pl.multiple_of(c * deep + SUB, SUB), deep)],
            dst_ref=held.at[slot, pl.ds(pl.multiple_of(c * deep, SUB), deep)],
            send_sem=detour_sem.at[0, p, c],
            recv_sem=detour_sem.at[1, p, c],
            device_id=(gg, relay, gy),
            device_id_type=pl.DeviceIdType.MESH,
        )

    def onward(path, p, c, slot):
        _, _, end, _, row = path
        return pltpu.make_async_remote_copy(
            src_ref=held.at[slot, pl.ds(pl.multiple_of(c * deep, SUB), deep)],
            dst_ref=field.at[p, row, pl.ds(pl.multiple_of(c * deep + SUB, SUB), deep)],
            send_sem=detour_sem.at[2, p, c],
            recv_sem=detour_sem.at[3, p, c],
            device_id=(gg, end, gy),
            device_id_type=pl.DeviceIdType.MESH,
        )

    def forward(message):
        slot = message // chunks
        c = message % chunks
        p = slot % 2
        for path in detours:
            @pl.when(gx == path[1])
            def _():
                @pl.when(slot >= 2)
                def _():
                    onward(path, p, c, slot).wait_send()

                away(path, p, c, slot).wait_recv()
                onward(path, p, c, slot).start()

    def start(p, c, slot):
        for path in detours:
            @pl.when(gx == path[0])
            def _():
                away(path, p, c, slot).start()
        each(1, lambda i, span: copy_of(i, p, c, span).start())

    def finish_recv(p, c):
        for path in detours:
            @pl.when(gx == path[2])
            def _():
                onward(path, p, c, 0).wait_recv()
        each(-1, lambda i, span: copy_of(i, p, c, span).wait_recv())

    def finish_send(p, c):
        for path in detours:
            @pl.when(gx == path[0])
            def _():
                away(path, p, c, 0).wait_send()
        each(1, lambda i, span: copy_of(i, p, c, span).wait_send())

    for p in range(2):
        for r, d in ((0, -1), (rows + 2, 1)):
            @pl.when(jnp.logical_not(there(d, 0)))
            def _():
                field[p, r : r + 2] = jnp.zeros((2, layers + 2 * SUB, width), jnp.float32)
        for r in range(2, rows + 2):
            for s in (0, SUB + layers):
                field[p, r, s : s + SUB] = jnp.zeros((SUB, width), jnp.float32)
        for ref, d in ((rim_left, -1), (rim_right, 1)):
            @pl.when(jnp.logical_not(there(0, d)))
            def _():
                ref[p] = jnp.zeros(ref.shape[1:], jnp.float32)
        for i in range(4):
            @pl.when(jnp.logical_not(there(-sides[4 + i][0], -sides[4 + i][1])))
            def _():
                for c in range(chunks):
                    cornered[p, c, i] = jnp.zeros((1, LANES), jnp.float32)

    barrier = pltpu.get_barrier_semaphore()

    def greet(device):
        pl.semaphore_signal(
            barrier, inc=1, device_id=device, device_id_type=pl.DeviceIdType.MESH
        )

    greet((1 - gg, gx, gy))
    for o in range(1, nx):
        greet((gg, lax.rem(gx + o, nx), gy))
    for o in range(1, ny):
        greet((gg, gx, lax.rem(gy + o, ny)))
    met = jnp.int32(1 + nx - 1 + ny - 1)
    for dx, dy in sides[4:]:
        @pl.when(there(dx, dy))
        def _():
            greet(at(dx, dy))
        met = met + jnp.where(there(dx, dy), 1, 0).astype(jnp.int32)

    lane = lax.broadcasted_iota(jnp.int32, (SUB, LANES), 1)
    sub = lax.broadcasted_iota(jnp.int32, (SUB, width), 0)

    tile_row = lax.broadcasted_iota(jnp.int32, (SUB, LANES), 0)

    def spot(i, t):
        return lane == (i * per + t) * SUB + tile_row

    def pack_row(x, value, tile, t, corners):
        first, last = value[:, :LANES], value[:, width - LANES :]
        low = first if x == 0 else pltpu.roll(first, 2 * x, 1)
        high = pltpu.roll(last, (two + 2 * x - LANES + 2) % LANES, 1)
        tile = jnp.where((lane >= 2 * x) & (lane < 2 * x + 2), low, tile)
        tile = jnp.where((lane >= two + 2 * x) & (lane < two + 2 * x + 2), high, tile)
        for i, (at_x, y) in enumerate(
            ((0, 0), (rows - 1, 0), (0, width - 1), (rows - 1, width - 1))
        ):
            if x == at_x:
                column = jnp.broadcast_to(value[:, y : y + 1], (SUB, LANES))
                corners = jnp.where(spot(i, t), column, corners)
        return tile, corners

    def put_corner(p, c, corners):
        corner[p, c] = jnp.sum(corners, axis=0, keepdims=True)

    ice_cells = ice[...].astype(jnp.float32)
    ground_cells = grounded[...].astype(jnp.float32)
    ocean = jnp.where(is_ice, 0.0, 1.0).astype(jnp.float32)
    active = ice_cells * (1.0 - ocean * ground_cells)
    friction = (1.0 - ocean) * friction_gain * ground_cells * ice_cells

    def wide(array, x):
        return jnp.broadcast_to(array[x : x + 1, :], (SUB, width))

    blank = jnp.zeros((SUB, LANES), jnp.float32)
    zero = jnp.zeros((SUB, width), jnp.float32)

    def first_pass(c, sums):
        @pl.when(c >= lag)
        def _():
            forward(c - lag)

        corners = blank
        for t in range(per):
            j = c * per + t
            ls = pl.ds(pl.multiple_of(j * SUB, SUB), SUB)
            tile, after = blank, []
            for x in range(rows):
                value = jnp.sqrt(conduct[x, ls, :]) * wide(active, x)
                coupling[x, ls, :] = value
                field[0, x + 2, pl.ds(pl.multiple_of(j * SUB + SUB, SUB), SUB), :] = value
                tile, corners = pack_row(x, value, tile, t, corners)
                after.append(sums[x] + force[x, ls, :])
            sums = tuple(after)
            pack[0, ls, :] = tile
        put_corner(0, c, corners)
        start(0, c, 0)
        return sums

    pl.semaphore_wait(barrier, met)
    sums = lax.fori_loop(0, chunks, first_pass, (zero,) * rows)
    for x in range(rows):
        mean = jnp.sum(sums[x], axis=0, keepdims=True) * (1.0 / layers)
        share[0, x : x + 1, :] = active[x : x + 1, :] * mean
        share[1, x : x + 1, :] = jnp.where(
            is_ice, coupling[x, 0:1, :], coupling[x, layers - 1 : layers, :]
        )

    to_partner = pltpu.make_async_remote_copy(
        src_ref=share,
        dst_ref=shared,
        send_sem=share_sem.at[0],
        recv_sem=share_sem.at[1],
        device_id=(1 - gg, gx, gy),
        device_id_type=pl.DeviceIdType.MESH,
    )
    to_partner.start()

    def spread_block(p, c, t):
        j = c * per + t
        here = pl.ds(pl.multiple_of(j * SUB + SUB, SUB), SUB)
        below = pl.ds(pl.multiple_of(j * SUB, SUB), SUB)
        above = pl.ds(pl.multiple_of(j * SUB + 2 * SUB, SUB), SUB)
        from_right, from_left = rim_right[p, below, :], rim_left[p, below, :]

        def column(i):
            row = jnp.broadcast_to(cornered[p, c, i], (SUB, LANES))
            return jnp.sum(jnp.where(spot(i, t), row, 0.0), axis=1, keepdims=True)

        def rim(x):
            right = from_right if x == 0 else pltpu.roll(from_right, LANES - 2 * x, 1)
            left = pltpu.roll(from_left, (LANES - 2 - two - 2 * x) % LANES, 1)
            return jnp.where(lane < LANES // 2, right, left)

        def line(x):
            if x == 0:
                edge = jnp.where(lane < LANES // 2, column(1), column(3))
            elif x == rows + 1:
                edge = jnp.where(lane < LANES // 2, column(0), column(2))
            else:
                edge = rim(x - 1)
            value = field[p, x + 1, here, :]
            return [value[:, l : l + LANES] for l in range(0, width, LANES)] + [edge]

        def shifted(tiles_in, by):
            count = len(tiles_in) - 1
            out = []
            for i in range(count):
                before, own, after = tiles_in[i - 1], tiles_in[i], tiles_in[i + 1]
                up = pltpu.roll(jnp.where(lane >= LANES - by, before, own), by, 1)
                down = pltpu.roll(jnp.where(lane < by, after, own), LANES - by, 1)
                out.append(up + down)
            return jnp.concatenate(out, axis=1)

        e = [line(0), line(1)]
        for x in range(rows):
            e.append(line(x + 2))
            beside = [a + b for a, b in zip(e[x], e[x + 2])]
            h = [a + cross_weight * b for a, b in zip(e[x + 1], beside)]
            mine = field[p, x + 2, here, :]
            up = pltpu.roll(jnp.where(sub == 0, field[p, x + 2, above, :], mine), SUB - 1, 0)
            down = pltpu.roll(jnp.where(sub == SUB - 1, field[p, x + 2, below, :], mine), 1, 0)
            yield (
                shifted(h, 1)
                + jnp.concatenate(beside[:-1], axis=1)
                + far_weight
                * (shifted(e[x + 1], 2) + (field[p, x, here, :] + field[p, x + 4, here, :]))
                + vertical_weight * (up + down)
            )

    def fold(value):
        return functools.reduce(
            lambda s, t: s + t, [value[:, c : c + LANES] for c in range(0, width, LANES)]
        )

    to_partner.wait_recv()
    term = active * (shared[1] * shared[0])

    edge = jnp.where(is_ice, 0, layers - 1).astype(jnp.int32)

    def zeroth(c, acc):
        forward(chunks + c - lag)
        finish_recv(0, c)
        corners = blank
        for t in range(per):
            j = c * per + t
            ls = pl.ds(pl.multiple_of(j * SUB, SUB), SUB)
            layer = sub + j * SUB
            at_edge = layer == edge
            at_bottom = layer == 0
            tile = blank
            for x, around in enumerate(list(spread_block(0, c, t))):
                own = coupling[x, ls, :]
                diag = (
                    extra[x, ls, :] + jnp.where(at_bottom, wide(friction, x), 0.0) + own * around
                )
                inverse = 1.0 / diag
                source = wide(active, x) * force[x, ls, :] + jnp.where(at_edge, wide(term, x), 0.0)
                vector = inverse * source
                diagonal[x, ls, :] = diag
                scaled[x, ls, :] = inverse * own
                basis[0, x, ls, :] = zero
                basis[1, x, ls, :] = vector
                value = own * vector
                field[1, x + 2, pl.ds(pl.multiple_of(j * SUB + SUB, SUB), SUB), :] = value
                tile, corners = pack_row(x, value, tile, t, corners)
                acc = acc + source * vector
            pack[1, ls, :] = tile
        put_corner(1, c, corners)
        start(1, c, 1)
        return acc

    partial[0] = fold(lax.fori_loop(0, chunks, zeroth, zero))
    partial[1] = blank
    to_partner.wait_send()

    def step(k, carry):
        p = lax.rem(k, 2)
        q = 1 - p
        gain = jnp.where(k == 1, 1.0, 2.0).astype(jnp.float32)

        def block(c, accs):
            own_acc, cross_acc = accs
            message = (k + 1) * chunks + c - lag

            @pl.when(message < (ITERS + 1) * chunks)
            def _():
                forward(message)

            finish_recv(p, c)
            finish_send(q, c)
            corners = blank
            for t in range(per):
                j = c * per + t
                ls = pl.ds(pl.multiple_of(j * SUB, SUB), SUB)
                tile = blank
                vectors, values = [], []
                for x, around in enumerate(list(spread_block(p, c, t))):
                    vector = gain * (scaled[x, ls, :] * around) - basis[k - 1, x, ls, :]
                    weighted = diagonal[x, ls, :] * vector
                    value = coupling[x, ls, :] * vector
                    own_acc = own_acc + weighted * vector
                    cross_acc = cross_acc + weighted * basis[k, x, ls, :]
                    tile, corners = pack_row(x, value, tile, t, corners)
                    vectors.append(vector)
                    values.append(value)
                after = pl.ds(pl.multiple_of(j * SUB + SUB, SUB), SUB)
                for x in range(rows):
                    basis[k + 1, x, ls, :] = vectors[x]
                    field[q, x + 2, after, :] = values[x]
                pack[q, ls, :] = tile
            put_corner(q, c, corners)

            @pl.when(k < ITERS)
            def _():
                start(q, c, k + 1)

            return own_acc, cross_acc

        own_acc, cross_acc = lax.fori_loop(0, chunks, block, (zero, zero))
        partial[2 * k] = fold(own_acc)
        partial[2 * k + 1] = fold(cross_acc)
        return carry

    lax.fori_loop(1, ITERS + 1, step, 0)

    def settle(c, carry):
        finish_send(ITERS % 2, c)
        for path in detours:
            @pl.when(gx == path[1])
            def _():
                for p in range(2):
                    onward(path, p, c, 0).wait_send()
        return carry

    lax.fori_loop(0, chunks, settle, 0)

    count = 2 * ITERS + 2

    def total(own, slots, n, me, axis, sends, recvs):
        slots[me] = own
        copies = []
        for o in range(1, n):
            peer = lax.rem(me + o, n)
            device = (gg, peer, gy) if axis == "gx" else (gg, gx, peer)
            copy = pltpu.make_async_remote_copy(
                src_ref=slots.at[me],
                dst_ref=slots.at[me],
                send_sem=sends.at[o - 1],
                recv_sem=recvs.at[o - 1],
                device_id=device,
                device_id_type=pl.DeviceIdType.MESH,
            )
            copy.start()
            copies.append(copy)
        for copy in copies:
            copy.wait_recv()
        result = slots[0]
        for o in range(1, n):
            result = result + slots[o]
        for copy in copies:
            copy.wait_send()
        return result

    own = jnp.concatenate(
        [jnp.sum(partial[m], axis=0, keepdims=True) for m in range(count)]
        + [jnp.zeros((2 * SUB - count, LANES), jnp.float32)],
        axis=0,
    )
    own = total(own, sum_x, nx, gx, "gx", sx_send, sx_recv)
    own = total(own, sum_y, ny, gy, "gy", sy_send, sy_recv)
    sums = jnp.sum(own, axis=1, keepdims=True)
    dots = [jnp.broadcast_to(sums[m : m + 1, :], (SUB, LANES)) for m in range(count)]
    moments = [dots[0], dots[3]]
    for k in range(1, ITERS + 1):
        if k > 1:
            moments.append(2.0 * dots[2 * k + 1] - moments[1])
        moments.append(2.0 * dots[2 * k] - moments[0])
    iterate, left = coefficients(moments)

    def widen(value):
        return jnp.concatenate([value] * (width // LANES), axis=1)

    iterate, left = [widen(v) for v in iterate], [widen(v) for v in left]

    def last(j, carry):
        ls = pl.ds(pl.multiple_of(j * SUB, SUB), SUB)
        for x in range(rows):
            us = [basis[k + 1, x, ls, :] for k in range(ITERS + 1)]
            out_x[x, ls, :] = functools.reduce(
                lambda s, t: s + t, [a * u for a, u in zip(iterate, us)]
            )
            out_r[x, ls, :] = diagonal[x, ls, :] * functools.reduce(
                lambda s, t: s + t, [a * u for a, u in zip(left, us)]
            )
        return carry

    lax.fori_loop(0, tiles, last, 0)


def on_device(nx, ny, forcing, conduct, diag_add, ice_mask, grounded):
    def turned(a):
        return jnp.transpose(a[0].astype(jnp.float32), (1, 0, 2))

    _, layers, rows, width = forcing.shape
    tiles = layers // SUB
    chunks = tiles // next(t for t in CHUNK_TILES if tiles % t == 0)
    f32 = jnp.float32
    block = jax.ShapeDtypeStruct((rows, layers, width), f32)
    vmem = pl.BlockSpec(memory_space=pltpu.VMEM)
    dma = pltpu.SemaphoreType.DMA
    out_x, out_r = pl.pallas_call(
        functools.partial(kernel, (nx, ny)),
        out_shape=(block, block),
        in_specs=[vmem] * 5,
        out_specs=(vmem, vmem),
        scratch_shapes=[
            pltpu.VMEM((2, rows + 4, layers + 2 * SUB, width), f32),
            pltpu.VMEM((2, layers, LANES), f32),
            pltpu.VMEM((2, layers, LANES), f32),
            pltpu.VMEM((2, layers, LANES), f32),
            pltpu.VMEM((2, chunks, 1, LANES), f32),
            pltpu.VMEM((2, chunks, 4, 1, LANES), f32),
            pltpu.VMEM((ITERS + 1, layers, width), f32),
            pltpu.VMEM((ITERS + 2, rows, layers, width), f32),
            pltpu.VMEM((rows, layers, width), f32),
            pltpu.VMEM((rows, layers, width), f32),
            pltpu.VMEM((rows, layers, width), f32),
            pltpu.VMEM((2, rows, width), f32),
            pltpu.VMEM((2, rows, width), f32),
            pltpu.VMEM((2 * ITERS + 2, SUB, LANES), f32),
            pltpu.VMEM((nx, 2 * SUB, LANES), f32),
            pltpu.VMEM((ny, 2 * SUB, LANES), f32),
            dma((2, chunks, 8)),
            dma((2, chunks, 8)),
            dma((2,)),
            dma((4, 2, chunks)),
            dma((nx - 1,)),
            dma((nx - 1,)),
            dma((ny - 1,)),
            dma((ny - 1,)),
        ],
        compiler_params=pltpu.CompilerParams(
            collective_id=0, has_side_effects=True, vmem_limit_bytes=40 * 1024 * 1024
        ),
        name="krylov",
    )(turned(forcing), turned(conduct), turned(diag_add), ice_mask, grounded)
    return tuple(jnp.transpose(o, (1, 0, 2))[None] for o in (out_x, out_r))


def solution(mesh):
    spec = P("group", None, "gx", "gy")
    flat = P("gx", "gy")
    return jax.shard_map(
        functools.partial(on_device, mesh.shape["gx"], mesh.shape["gy"]),
        mesh=mesh,
        in_specs=(spec, spec, spec, flat, flat),
        out_specs=(spec, spec),
        check_vma=False,
    )
```

profile of v0, /device:TPU:0, one launch (start us, length us, event | category | flops | bytes accessed | tf_op | source)
XLA Modules:
  0.0 67.3 jit_solution(7373741890367117518)
XLA Ops:
  0.6 0.0 copy-start.2
  0.6 0.0 copy-start.3
  0.6 1.4 %copy.15 = f32[1,80,8,256]{3,1,2,0:T(8,128)S(1)} copy(f32[1,80,8,256]{3,2,1,0:T(8,128)} %param.5) | data formatting | bytes 1310720 | tf_op args[0]
  2.0 0.0 copy-done.2
  2.0 0.0 copy-done.3
  2.0 0.0 copy-start
  2.0 0.0 copy-start.1
  2.1 0.1 convert_bitcast_fusion
  2.2 0.5 copy-done
  2.7 0.0 copy-done.1
  2.8 62.1 %krylov.1 = (f32[8,80,256]{2,1,0:T(8,128)S(1)}, f32[8,80,256]{2,1,0:T(8,128)S(1)}) custom-call(f32[8,80,256]{2,1,0:T(8,128)S(1)} %bitcast.21, f32[8,80,256]{2,1,0:T(8,128)S(1)} %get-tuple-element.9.conduct, f32[8,80,256]{2,1,0:T(8,128)S(1)} %get-tuple-element.8.extra, s32[8,256]{1,0:T(8,128)S(1)} %copy-done, s32[8,256]{1,0:T(8,128)S(1)} %copy-done.1), custom_call_target="tpu_custom_call" | custom-call | tf_op jit(solution)/shard_map/krylov/pallas_call | solution.py:582
  64.9 1.2 %copy.10 = f32[1,80,8,256]{3,2,1,0:T(8,128)} copy(f32[1,80,8,256]{3,1,2,0:T(8,128)S(1)} %bitcast.23) | data formatting | bytes 1310720
  66.1 1.2 %copy.11 = f32[1,80,8,256]{3,2,1,0:T(8,128)} copy(f32[1,80,8,256]{3,1,2,0:T(8,128)S(1)} %bitcast.22) | data formatting | bytes 1310720
Async XLA Ops:
  0.6 1.4 %copy-start.2 = (bf16[1,80,8,256]{3,2,1,0:T(8,128)(2,1)S(1)}, bf16[1,80,8,256]{3,2,1,0:T(8,128)(2,1)}, u32[]{:S(2)}) copy-start(bf16[1,80,8,256]{3,2,1,0:T(8,128)(2,1)} %param.7) | copy-start | bytes 983044
  0.6 1.4 %copy-start.3 = (bf16[1,80,8,256]{3,2,1,0:T(8,128)(2,1)S(1)}, bf16[1,80,8,256]{3,2,1,0:T(8,128)(2,1)}, u32[]{:S(2)}) copy-start(bf16[1,80,8,256]{3,2,1,0:T(8,128)(2,1)} %param.6) | copy-start | bytes 983044
  2.0 0.7 %copy-start = (s32[8,256]{1,0:T(8,128)S(1)}, s32[8,256]{1,0:T(8,128)}, u32[]{:S(2)}) copy-start(s32[8,256]{1,0:T(8,128)} %ice.1) | copy-start | bytes 24580
  2.0 0.7 %copy-start.1 = (s32[8,256]{1,0:T(8,128)S(1)}, s32[8,256]{1,0:T(8,128)}, u32[]{:S(2)}) copy-start(s32[8,256]{1,0:T(8,128)} %grounded.1) | copy-start | bytes 24580
where the time goes:
time: 67.5 us; the launch traced here: 67.3 us
  Pallas kernels  62.1 us (92%)
  local copies, waits for them, and re-layouts  4.36 us (6%)
  between operations  0.7 us (1%)
    pallas_call x1, Pallas kernels, on_device(): pl.pallas_call(functools.partial(kernel, (nx, ny)), out_shape=(block, blo...  62.1 us
    unnamed x11, local copies, waits for them, and re-layouts  4.36 us

commit v1 on v0

--- a/solution.py
+++ b/solution.py
@@ -155,8 +155,9 @@
             device_id_type=pl.DeviceIdType.MESH,
         )
 
-    detours = ((1, 3, 2, rows + 1, 1), (2, 0, 1, 3, rows + 3)) if nx == 4 else ()
-    lag = min(4, chunks - 1)
+    detours = ((1, 3, 2, rows, 0), (2, 0, 1, 2, rows + 2)) if nx == 4 else ()
+    relayed = gg == 1
+    lag = min(3, chunks - 1)
 
     def each(toward, act):
         for i, (dx, dy) in enumerate(sides):
@@ -164,11 +165,7 @@
             if i < 2 and detours:
                 split = gx == ((2 - i) if toward > 0 else (1 + i))
 
-                @pl.when(split)
-                def _():
-                    act(i, 1)
-
-                ok = ok & jnp.logical_not(split)
+                ok = ok & jnp.logical_not(split & relayed)
 
             @pl.when(ok)
             def _():
@@ -177,8 +174,8 @@
     def away(path, p, c, slot):
         origin, relay, _, row, _ = path
         return pltpu.make_async_remote_copy(
-            src_ref=field.at[p, row, pl.ds(pl.multiple_of(c * deep + SUB, SUB), deep)],
-            dst_ref=held.at[slot, pl.ds(pl.multiple_of(c * deep, SUB), deep)],
+            src_ref=field.at[p, row : row + 2, pl.ds(pl.multiple_of(c * deep + SUB, SUB), deep)],
+            dst_ref=held.at[slot, :, pl.ds(pl.multiple_of(c * deep, SUB), deep)],
             send_sem=detour_sem.at[0, p, c],
             recv_sem=detour_sem.at[1, p, c],
             device_id=(gg, relay, gy),
@@ -188,8 +185,8 @@
     def onward(path, p, c, slot):
         _, _, end, _, row = path
         return pltpu.make_async_remote_copy(
-            src_ref=held.at[slot, pl.ds(pl.multiple_of(c * deep, SUB), deep)],
-            dst_ref=field.at[p, row, pl.ds(pl.multiple_of(c * deep + SUB, SUB), deep)],
+            src_ref=held.at[slot, :, pl.ds(pl.multiple_of(c * deep, SUB), deep)],
+            dst_ref=field.at[p, row : row + 2, pl.ds(pl.multiple_of(c * deep + SUB, SUB), deep)],
             send_sem=detour_sem.at[2, p, c],
             recv_sem=detour_sem.at[3, p, c],
             device_id=(gg, end, gy),
@@ -201,7 +198,7 @@
         c = message % chunks
         p = slot % 2
         for path in detours:
-            @pl.when(gx == path[1])
+            @pl.when((gx == path[1]) & relayed)
             def _():
                 @pl.when(slot >= 2)
                 def _():
@@ -212,21 +209,21 @@
 
     def start(p, c, slot):
         for path in detours:
-            @pl.when(gx == path[0])
+            @pl.when((gx == path[0]) & relayed)
             def _():
                 away(path, p, c, slot).start()
         each(1, lambda i, span: copy_of(i, p, c, span).start())
 
     def finish_recv(p, c):
         for path in detours:
-            @pl.when(gx == path[2])
+            @pl.when((gx == path[2]) & relayed)
             def _():
                 onward(path, p, c, 0).wait_recv()
         each(-1, lambda i, span: copy_of(i, p, c, span).wait_recv())
 
     def finish_send(p, c):
         for path in detours:
-            @pl.when(gx == path[0])
+            @pl.when((gx == path[0]) & relayed)
             def _():
                 away(path, p, c, 0).wait_send()
         each(1, lambda i, span: copy_of(i, p, c, span).wait_send())
@@ -497,7 +494,7 @@
     def settle(c, carry):
         finish_send(ITERS % 2, c)
         for path in detours:
-            @pl.when(gx == path[1])
+            @pl.when((gx == path[1]) & relayed)
             def _():
                 for p in range(2):
                     onward(path, p, c, 0).wait_send()
@@ -591,7 +588,7 @@
             pltpu.VMEM((2, layers, LANES), f32),
             pltpu.VMEM((2, chunks, 1, LANES), f32),
             pltpu.VMEM((2, chunks, 4, 1, LANES), f32),
-            pltpu.VMEM((ITERS + 1, layers, width), f32),
+            pltpu.VMEM((ITERS + 1, 2, layers, width), f32),
             pltpu.VMEM((ITERS + 2, rows, layers, width), f32),
             pltpu.VMEM((rows, layers, width), f32),
             pltpu.VMEM((rows, layers, width), f32),

time: 67.5 us -> 65.1 us (0.964)
  Pallas kernels: 62.1 us -> 59.6 us
    pallas_call x1, Pallas kernels: 62.1 us -> 59.6 us  [on_device(): pl.pallas_call(functools.partial(kernel, (nx, ny)), out_shape=(block, blo...]
where the time goes in v1:
time: 65.1 us; the launch traced here: 64.8 us
  Pallas kernels  59.6 us (92%)
  local copies, waits for them, and re-layouts  4.36 us (7%)
  between operations  0.7 us (1%)
    pallas_call x1, Pallas kernels, on_device(): pl.pallas_call(functools.partial(kernel, (nx, ny)), out_shape=(block, blo...  59.6 us
    unnamed x11, local copies, waits for them, and re-layouts  4.36 us

profile of v1, /device:TPU:0, one launch (start us, length us, event | category | flops | bytes accessed | tf_op | source)
XLA Modules:
  0.0 64.8 jit_solution(8055586005725444510)
XLA Ops:
  0.6 0.0 copy-start.2
  0.6 0.0 copy-start.3
  0.6 1.4 %copy.15 = f32[1,80,8,256]{3,1,2,0:T(8,128)S(1)} copy(f32[1,80,8,256]{3,2,1,0:T(8,128)} %param.5) | data formatting | bytes 1310720 | tf_op args[0]
  2.0 0.0 copy-done.2
  2.0 0.0 copy-done.3
  2.0 0.0 copy-start
  2.0 0.0 copy-start.1
  2.1 0.1 convert_bitcast_fusion
  2.2 0.5 copy-done
  2.7 0.0 copy-done.1
  2.8 59.6 %krylov.1 = (f32[8,80,256]{2,1,0:T(8,128)S(1)}, f32[8,80,256]{2,1,0:T(8,128)S(1)}) custom-call(f32[8,80,256]{2,1,0:T(8,128)S(1)} %bitcast.21, f32[8,80,256]{2,1,0:T(8,128)S(1)} %get-tuple-element.9.conduct, f32[8,80,256]{2,1,0:T(8,128)S(1)} %get-tuple-element.8.extra, s32[8,256]{1,0:T(8,128)S(1)} %copy-done, s32[8,256]{1,0:T(8,128)S(1)} %copy-done.1), custom_call_target="tpu_custom_call" | custom-call | tf_op jit(solution)/shard_map/krylov/pallas_call | solution.py:579
  62.4 1.2 %copy.10 = f32[1,80,8,256]{3,2,1,0:T(8,128)} copy(f32[1,80,8,256]{3,1,2,0:T(8,128)S(1)} %bitcast.23) | data formatting | bytes 1310720
  63.6 1.2 %copy.11 = f32[1,80,8,256]{3,2,1,0:T(8,128)} copy(f32[1,80,8,256]{3,1,2,0:T(8,128)S(1)} %bitcast.22) | data formatting | bytes 1310720
Async XLA Ops:
  0.6 1.4 %copy-start.2 = (bf16[1,80,8,256]{3,2,1,0:T(8,128)(2,1)S(1)}, bf16[1,80,8,256]{3,2,1,0:T(8,128)(2,1)}, u32[]{:S(2)}) copy-start(bf16[1,80,8,256]{3,2,1,0:T(8,128)(2,1)} %param.7) | copy-start | bytes 983044
  0.6 1.4 %copy-start.3 = (bf16[1,80,8,256]{3,2,1,0:T(8,128)(2,1)S(1)}, bf16[1,80,8,256]{3,2,1,0:T(8,128)(2,1)}, u32[]{:S(2)}) copy-start(bf16[1,80,8,256]{3,2,1,0:T(8,128)(2,1)} %param.6) | copy-start | bytes 983044
  2.0 0.7 %copy-start = (s32[8,256]{1,0:T(8,128)S(1)}, s32[8,256]{1,0:T(8,128)}, u32[]{:S(2)}) copy-start(s32[8,256]{1,0:T(8,128)} %ice.1) | copy-start | bytes 24580
  2.0 0.7 %copy-start.1 = (s32[8,256]{1,0:T(8,128)S(1)}, s32[8,256]{1,0:T(8,128)}, u32[]{:S(2)}) copy-start(s32[8,256]{1,0:T(8,128)} %grounded.1) | copy-start | bytes 24580

commit v2 on v1

--- a/solution.py
+++ b/solution.py
@@ -21,7 +21,12 @@
     def gram(j, k):
         return 0.5 * (moments[j + k] + moments[abs(j - k)])
 
-    table = {(j, k): gram(j, k) for j in range(ITERS + 1) for k in range(j, ITERS + 1)}
+    table = {
+        (j, k): gram(j, k)
+        for j in range(ITERS + 1)
+        for k in range(j, ITERS + 1)
+        if j + k < len(moments)
+    }
 
     def form(a, b):
         terms = []
@@ -53,6 +58,10 @@
             (direction[k] - moved[k]) if k < len(direction) else -moved[k]
             for k in range(len(moved))
         ]
+        if iteration + 1 == ITERS:
+            table[iteration, ITERS] = 0.5 * moments[1]
+            slope = 0.5 * direction[-1] * applied[-1]
+            return iterate, left, direction, applied, norm_now, form(direction, applied), slope
         step = norm_now / form(direction, applied)
         iterate = [
             (iterate[k] if k < len(iterate) else 0.0) + step * direction[k]
@@ -62,26 +71,27 @@
             (left[k] - step * applied[k]) if k < len(left) else -step * applied[k]
             for k in range(len(applied))
         ]
-        if iteration + 1 < ITERS:
-            norm_next = form(left, left)
-            ratio = norm_next / norm_now
-            direction = [
-                left[k] + (ratio * direction[k] if k < len(direction) else 0.0)
-                for k in range(len(left))
-            ]
-            norm_now = norm_next
-    return iterate, left
+        norm_next = form(left, left)
+        ratio = norm_next / norm_now
+        direction = [
+            left[k] + (ratio * direction[k] if k < len(direction) else 0.0)
+            for k in range(len(left))
+        ]
+        norm_now = norm_next
 
 
 def kernel(
     sizes,
-    force,
+    force_hbm,
     conduct,
     extra,
     ice,
     grounded,
     out_x,
+    out_p,
     out_r,
+    out_q,
+    out_s,
     field,
     pack,
     rim_right,
@@ -96,19 +106,23 @@
     share,
     shared,
     partial,
-    sum_x,
-    sum_y,
+    sum_early,
+    sum_all,
     send_sem,
     recv_sem,
     share_sem,
     detour_sem,
-    sx_send,
-    sx_recv,
-    sy_send,
-    sy_recv,
+    se_send,
+    se_recv,
+    sa_send,
+    sa_recv,
+    force,
+    force_sem,
 ):
     nx, ny = sizes
-    rows, layers, width = force.shape
+    rows, layers, width = conduct.shape
+    fetch = pltpu.make_async_copy(force_hbm, force, force_sem)
+    fetch.start()
     tiles = layers // SUB
     chunks = corner.shape[1]
     per = tiles // chunks
@@ -248,22 +262,39 @@
 
     barrier = pltpu.get_barrier_semaphore()
 
+    def peers_all():
+        me = gx * ny + gy
+        out = []
+        for o in range(1, nx * ny):
+            peer = lax.rem(me + o, nx * ny)
+            out.append((gg, peer // ny, lax.rem(peer, ny)))
+        return out
+
     def greet(device):
         pl.semaphore_signal(
             barrier, inc=1, device_id=device, device_id_type=pl.DeviceIdType.MESH
         )
 
     greet((1 - gg, gx, gy))
-    for o in range(1, nx):
-        greet((gg, lax.rem(gx + o, nx), gy))
-    for o in range(1, ny):
-        greet((gg, gx, lax.rem(gy + o, ny)))
-    met = jnp.int32(1 + nx - 1 + ny - 1)
-    for dx, dy in sides[4:]:
-        @pl.when(there(dx, dy))
-        def _():
-            greet(at(dx, dy))
-        met = met + jnp.where(there(dx, dy), 1, 0).astype(jnp.int32)
+    if max(nx, ny) < ITERS:
+        met = jnp.int32(1)
+        for dx, dy in sides:
+            @pl.when(there(dx, dy))
+            def _():
+                greet(at(dx, dy))
+            met = met + jnp.where(there(dx, dy), 1, 0).astype(jnp.int32)
+        for origin, relay, end, _, _ in detours:
+            for one, other in ((origin, relay), (relay, end)):
+                for here, peer in ((one, other), (other, one)):
+                    if abs(here - peer) > 1:
+                        @pl.when(gx == here)
+                        def _():
+                            greet((gg, peer, gy))
+                        met = met + jnp.where(gx == here, 1, 0).astype(jnp.int32)
+    else:
+        for device in peers_all():
+            greet(device)
+        met = jnp.int32(nx * ny)
 
     lane = lax.broadcasted_iota(jnp.int32, (SUB, LANES), 1)
     sub = lax.broadcasted_iota(jnp.int32, (SUB, width), 0)
@@ -302,7 +333,7 @@
     blank = jnp.zeros((SUB, LANES), jnp.float32)
     zero = jnp.zeros((SUB, width), jnp.float32)
 
-    def first_pass(c, sums):
+    def first_pass(c, carry):
         @pl.when(c >= lag)
         def _():
             forward(c - lag)
@@ -311,24 +342,29 @@
         for t in range(per):
             j = c * per + t
             ls = pl.ds(pl.multiple_of(j * SUB, SUB), SUB)
-            tile, after = blank, []
+            tile = blank
             for x in range(rows):
                 value = jnp.sqrt(conduct[x, ls, :]) * wide(active, x)
                 coupling[x, ls, :] = value
                 field[0, x + 2, pl.ds(pl.multiple_of(j * SUB + SUB, SUB), SUB), :] = value
                 tile, corners = pack_row(x, value, tile, t, corners)
-                after.append(sums[x] + force[x, ls, :])
-            sums = tuple(after)
             pack[0, ls, :] = tile
         put_corner(0, c, corners)
         start(0, c, 0)
-        return sums
+        return carry
 
     pl.semaphore_wait(barrier, met)
-    sums = lax.fori_loop(0, chunks, first_pass, (zero,) * rows)
+    lax.fori_loop(0, chunks, first_pass, 0)
+    fetch.wait()
+
+    def gather(j, total):
+        for t in range(SUB):
+            total = total + force[j * SUB + t]
+        return total
+
+    total = lax.fori_loop(0, tiles, gather, jnp.zeros((rows, width), jnp.float32))
+    share[0] = active * (total * (1.0 / layers))
     for x in range(rows):
-        mean = jnp.sum(sums[x], axis=0, keepdims=True) * (1.0 / layers)
-        share[0, x : x + 1, :] = active[x : x + 1, :] * mean
         share[1, x : x + 1, :] = jnp.where(
             is_ice, coupling[x, 0:1, :], coupling[x, layers - 1 : layers, :]
         )
@@ -422,7 +458,7 @@
                     extra[x, ls, :] + jnp.where(at_bottom, wide(friction, x), 0.0) + own * around
                 )
                 inverse = 1.0 / diag
-                source = wide(active, x) * force[x, ls, :] + jnp.where(at_edge, wide(term, x), 0.0)
+                source = wide(active, x) * force[ls, x, :] + jnp.where(at_edge, wide(term, x), 0.0)
                 vector = inverse * source
                 diagonal[x, ls, :] = diag
                 scaled[x, ls, :] = inverse * own
@@ -440,6 +476,43 @@
     partial[0] = fold(lax.fori_loop(0, chunks, zeroth, zero))
     partial[1] = blank
     to_partner.wait_send()
+
+    lane_row = lax.broadcasted_iota(jnp.int32, (1, LANES), 1)
+
+    def copies(slots, me, devices, sends, recvs):
+        return [
+            pltpu.make_async_remote_copy(
+                src_ref=slots.at[me],
+                dst_ref=slots.at[me],
+                send_sem=sends.at[o],
+                recv_sem=recvs.at[o],
+                device_id=device,
+                device_id_type=pl.DeviceIdType.MESH,
+            )
+            for o, device in enumerate(devices)
+        ]
+
+    def row_of(slots):
+        return functools.reduce(lambda s, t: s + t, [slots[o] for o in range(slots.shape[0])])
+
+    def copies_early():
+        return copies(sum_early, gx * ny + gy, peers_all(), se_send, se_recv)
+
+    def early_start():
+        row = jnp.zeros((1, LANES), jnp.float32)
+        for m in range(2 * ITERS):
+            value = jnp.sum(partial[m], axis=0, keepdims=True)
+            value = jnp.sum(value, axis=1, keepdims=True)
+            row = jnp.where(lane_row == m, jnp.broadcast_to(value, (1, LANES)), row)
+        sum_early[gx * ny + gy] = row
+        for copy in copies_early():
+            copy.start()
+
+    def early_finish():
+        for copy in copies_early():
+            copy.wait_recv()
+        for copy in copies_early():
+            copy.wait_send()
 
     def step(k, carry):
         p = lax.rem(k, 2)
@@ -487,9 +560,18 @@
         own_acc, cross_acc = lax.fori_loop(0, chunks, block, (zero, zero))
         partial[2 * k] = fold(own_acc)
         partial[2 * k + 1] = fold(cross_acc)
+
+        @pl.when(k == ITERS - 1)
+        def _():
+            early_start()
+
         return carry
 
     lax.fori_loop(1, ITERS + 1, step, 0)
+    sum_all[gx * ny + gy] = jnp.sum(partial[2 * ITERS + 1], axis=0, keepdims=True)
+    to_all = copies(sum_all, gx * ny + gy, peers_all(), sa_send, sa_recv)
+    for copy in to_all:
+        copy.start()
 
     def settle(c, carry):
         finish_send(ITERS % 2, c)
@@ -502,67 +584,44 @@
 
     lax.fori_loop(0, chunks, settle, 0)
 
-    count = 2 * ITERS + 2
-
-    def total(own, slots, n, me, axis, sends, recvs):
-        slots[me] = own
-        copies = []
-        for o in range(1, n):
-            peer = lax.rem(me + o, n)
-            device = (gg, peer, gy) if axis == "gx" else (gg, gx, peer)
-            copy = pltpu.make_async_remote_copy(
-                src_ref=slots.at[me],
-                dst_ref=slots.at[me],
-                send_sem=sends.at[o - 1],
-                recv_sem=recvs.at[o - 1],
-                device_id=device,
-                device_id_type=pl.DeviceIdType.MESH,
-            )
-            copy.start()
-            copies.append(copy)
-        for copy in copies:
-            copy.wait_recv()
-        result = slots[0]
-        for o in range(1, n):
-            result = result + slots[o]
-        for copy in copies:
-            copy.wait_send()
-        return result
-
-    own = jnp.concatenate(
-        [jnp.sum(partial[m], axis=0, keepdims=True) for m in range(count)]
-        + [jnp.zeros((2 * SUB - count, LANES), jnp.float32)],
-        axis=0,
-    )
-    own = total(own, sum_x, nx, gx, "gx", sx_send, sx_recv)
-    own = total(own, sum_y, ny, gy, "gy", sy_send, sy_recv)
-    sums = jnp.sum(own, axis=1, keepdims=True)
-    dots = [jnp.broadcast_to(sums[m : m + 1, :], (SUB, LANES)) for m in range(count)]
+    early_finish()
+    total = row_of(sum_early)
+    dots = [jnp.broadcast_to(total[:, m : m + 1], (SUB, LANES)) for m in range(2 * ITERS)]
     moments = [dots[0], dots[3]]
-    for k in range(1, ITERS + 1):
+    for k in range(1, ITERS):
         if k > 1:
             moments.append(2.0 * dots[2 * k + 1] - moments[1])
         moments.append(2.0 * dots[2 * k] - moments[0])
-    iterate, left = coefficients(moments)
+    *lists, norm, fixed, slope = coefficients(moments)
 
     def widen(value):
         return jnp.concatenate([value] * (width // LANES), axis=1)
 
-    iterate, left = [widen(v) for v in iterate], [widen(v) for v in left]
+    iterate, left, direction, applied = [[widen(v) for v in values] for values in lists]
+
+    def combined(values, us):
+        return functools.reduce(lambda s, t: s + t, [a * u for a, u in zip(values, us)])
 
     def last(j, carry):
         ls = pl.ds(pl.multiple_of(j * SUB, SUB), SUB)
         for x in range(rows):
             us = [basis[k + 1, x, ls, :] for k in range(ITERS + 1)]
-            out_x[x, ls, :] = functools.reduce(
-                lambda s, t: s + t, [a * u for a, u in zip(iterate, us)]
-            )
-            out_r[x, ls, :] = diagonal[x, ls, :] * functools.reduce(
-                lambda s, t: s + t, [a * u for a, u in zip(left, us)]
-            )
+            diag = diagonal[x, ls, :]
+            out_x[ls, x, :] = combined(iterate, us)
+            out_p[ls, x, :] = combined(direction, us)
+            out_r[ls, x, :] = diag * combined(left, us)
+            out_q[ls, x, :] = diag * combined(applied, us)
         return carry
 
     lax.fori_loop(0, tiles, last, 0)
+
+    for copy in to_all:
+        copy.wait_recv()
+    cross = jnp.sum(row_of(sum_all), axis=1, keepdims=True)
+    cross = jnp.broadcast_to(cross, (SUB, LANES))
+    out_s[...] = widen(norm / (fixed + slope * (2.0 * cross - moments[1])))
+    for copy in to_all:
+        copy.wait_send()
 
 
 def on_device(nx, ny, forcing, conduct, diag_add, ice_mask, grounded):
@@ -576,11 +635,11 @@
     block = jax.ShapeDtypeStruct((rows, layers, width), f32)
     vmem = pl.BlockSpec(memory_space=pltpu.VMEM)
     dma = pltpu.SemaphoreType.DMA
-    out_x, out_r = pl.pallas_call(
+    out_x, out_p, out_r, out_q, out_s = pl.pallas_call(
         functools.partial(kernel, (nx, ny)),
-        out_shape=(block, block),
-        in_specs=[vmem] * 5,
-        out_specs=(vmem, vmem),
+        out_shape=(jax.ShapeDtypeStruct((layers, rows, width), f32),) * 4 + (jax.ShapeDtypeStruct((SUB, width), f32),),
+        in_specs=[pl.BlockSpec(memory_space=pl.ANY)] + [vmem] * 4,
+        out_specs=(vmem,) * 5,
         scratch_shapes=[
             pltpu.VMEM((2, rows + 4, layers + 2 * SUB, width), f32),
             pltpu.VMEM((2, layers, LANES), f32),
@@ -596,23 +655,27 @@
             pltpu.VMEM((2, rows, width), f32),
             pltpu.VMEM((2, rows, width), f32),
             pltpu.VMEM((2 * ITERS + 2, SUB, LANES), f32),
-            pltpu.VMEM((nx, 2 * SUB, LANES), f32),
-            pltpu.VMEM((ny, 2 * SUB, LANES), f32),
+            pltpu.VMEM((nx * ny, 1, LANES), f32),
+            pltpu.VMEM((nx * ny, 1, LANES), f32),
             dma((2, chunks, 8)),
             dma((2, chunks, 8)),
             dma((2,)),
             dma((4, 2, chunks)),
-            dma((nx - 1,)),
-            dma((nx - 1,)),
-            dma((ny - 1,)),
-            dma((ny - 1,)),
+            dma((nx * ny - 1,)),
+            dma((nx * ny - 1,)),
+            dma((nx * ny - 1,)),
+            dma((nx * ny - 1,)),
+            pltpu.VMEM((layers, rows, width), f32),
+            dma,
         ],
         compiler_params=pltpu.CompilerParams(
             collective_id=0, has_side_effects=True, vmem_limit_bytes=40 * 1024 * 1024
         ),
         name="krylov",
-    )(turned(forcing), turned(conduct), turned(diag_add), ice_mask, grounded)
-    return tuple(jnp.transpose(o, (1, 0, 2))[None] for o in (out_x, out_r))
+    )(forcing[0], turned(conduct), turned(diag_add), ice_mask, grounded)
+    step = out_s[:1]
+    solved, residual = out_x + step * out_p, out_r - step * out_q
+    return tuple(o[None] for o in (solved, residual))
 
 
 def solution(mesh):

time: 65.1 us -> 60.1 us (0.923)
  local copies, waits for them, and re-layouts: 4.36 us -> 0.02 us
  Pallas kernels: 59.6 us -> 56.8 us
  other arithmetic: 0.15 us -> 2.5 us
    unnamed x11 -> x6, local copies, waits for them, and re-layouts: 4.36 us -> 0.01 us
    pallas_call x1, Pallas kernels: 59.6 us -> 56.8 us  [on_device(): pl.pallas_call(functools.partial(kernel, (nx, ny)), out_shape=(jax.ShapeD...]
    broadcast_in_dim x0 -> x1, other arithmetic: none -> 1.22 us  [on_device(): return tuple((o[None] for o in (solved, residual)))]
    transpose x1, other arithmetic: 0.15 us -> 1.28 us  [turned(): return jnp.transpose(a[0].astype(jnp.float32), (1, 0, 2))]
where the time goes in v2:
time: 60.1 us; the launch traced here: 60 us
  Pallas kernels  56.8 us (95%)
  other arithmetic  2.5 us (4%)
  between operations  0.7 us (1%)
    pallas_call x1, Pallas kernels, on_device(): pl.pallas_call(functools.partial(kernel, (nx, ny)), out_shape=(jax.ShapeD...  56.8 us
    transpose x1, other arithmetic, turned(): return jnp.transpose(a[0].astype(jnp.float32), (1, 0, 2))  1.28 us
    broadcast_in_dim x1, other arithmetic, on_device(): return tuple((o[None] for o in (solved, residual)))  1.22 us

profile of v2, /device:TPU:0, one launch (start us, length us, event | category | flops | bytes accessed | tf_op | source)
XLA Modules:
  0.0 60.0 jit_solution(7564850459017040200)
XLA Ops:
  0.6 0.0 copy-start
  0.6 0.0 copy-start.1
  0.7 0.0 copy-start.2
  0.7 1.3 %convert_bitcast_fusion = (f32[8,80,256]{2,1,0:T(8,128)S(1)}, f32[8,80,256]{2,1,0:T(8,128)S(1)}) fusion(bf16[1,80,8,256]{3,2,1,0:T(8,128)(2,1)} %param.7, bf16[1,80,8,256]{3,2,1,0:T(8,128)(2,1)} %param.6), kind=kLoop, calls=%fused_computation | loop fusion | flops 327680 | bytes 1966080 | tf_op jit(solution)/shard_map/transpose | solution.py:629
  1.9 0.0 copy-done
  2.0 0.0 copy-done.1
  2.0 0.0 copy-done.2
  2.0 56.8 %krylov.1 = (f32[80,8,256]{2,1,0:T(8,128)S(1)}, f32[80,8,256]{2,1,0:T(8,128)S(1)}, f32[80,8,256]{2,1,0:T(8,128)S(1)}, f32[80,8,256]{2,1,0:T(8,128)S(1)}, f32[8,256]{1,0:T(8,128)S(1)}) custom-call(f32[80,8,256]{2,1,0:T(8,128)S(1)} %bitcast.16, f32[8,80,256]{2,1,0:T(8,128)S(1)} %get-tuple-element.15.conduct, f32[8,80,256]{2,1,0:T(8,128)S(1)} %get-tuple-element.14.extra, ...), custom_call_target="tpu_custom_call" | custom-call | tf_op jit(solution)/shard_map/krylov/pallas_call | solution.py:638
  58.7 1.2 %subtract_bitcast_fusion = (f32[1,80,8,256]{3,2,1,0:T(8,128)}, f32[1,80,8,256]{3,2,1,0:T(8,128)}) fusion(f32[80,8,256]{2,1,0:T(8,128)S(1)} %get-tuple-element.10, f32[80,8,256]{2,1,0:T(8,128)S(1)} %get-tuple-element.11, f32[256]{0:T(256)S(1)} %bitcast.17, f32[80,8,256]{2,1,0:T(8,128)S(1)} %get-tuple-element.7, f32[80,8,256]{2,1,0:T(8,128)S(1)} %get-tuple-element.9), kind=kLoop, calls=%fused_computation.2 | loop fusion | flops 655360 | bytes 3933184 | tf_op jit(solution)/shard_map/broadcast_in_dim | solution.py:678
  (1 shorter events, 0.0 us)
Async XLA Ops:
  0.6 1.3 %copy-start = (f32[1,80,8,256]{3,2,1,0:T(8,128)S(1)}, f32[1,80,8,256]{3,2,1,0:T(8,128)}, u32[]{:S(2)}) copy-start(f32[1,80,8,256]{3,2,1,0:T(8,128)} %param.5) | copy-start | bytes 1966084
  0.6 1.3 %copy-start.1 = (s32[8,256]{1,0:T(8,128)S(1)}, s32[8,256]{1,0:T(8,128)}, u32[]{:S(2)}) copy-start(s32[8,256]{1,0:T(8,128)} %ice.1) | copy-start | bytes 24580
  0.7 1.3 %copy-start.2 = (s32[8,256]{1,0:T(8,128)S(1)}, s32[8,256]{1,0:T(8,128)}, u32[]{:S(2)}) copy-start(s32[8,256]{1,0:T(8,128)} %grounded.1) | copy-start | bytes 24580

commit v3 on v2

--- a/solution.py
+++ b/solution.py
@@ -14,7 +14,7 @@
 friction_gain = 8.0
 SUB = 8
 LANES = 128
-CHUNK_TILES = (1,)
+CHUNK_TILES = (2, 1)
 
 
 def coefficients(moments):
@@ -82,7 +82,7 @@
 
 def kernel(
     sizes,
-    force_hbm,
+    force,
     conduct,
     extra,
     ice,
@@ -116,13 +116,9 @@
     se_recv,
     sa_send,
     sa_recv,
-    force,
-    force_sem,
 ):
     nx, ny = sizes
     rows, layers, width = conduct.shape
-    fetch = pltpu.make_async_copy(force_hbm, force, force_sem)
-    fetch.start()
     tiles = layers // SUB
     chunks = corner.shape[1]
     per = tiles // chunks
@@ -242,24 +238,6 @@
                 away(path, p, c, 0).wait_send()
         each(1, lambda i, span: copy_of(i, p, c, span).wait_send())
 
-    for p in range(2):
-        for r, d in ((0, -1), (rows + 2, 1)):
-            @pl.when(jnp.logical_not(there(d, 0)))
-            def _():
-                field[p, r : r + 2] = jnp.zeros((2, layers + 2 * SUB, width), jnp.float32)
-        for r in range(2, rows + 2):
-            for s in (0, SUB + layers):
-                field[p, r, s : s + SUB] = jnp.zeros((SUB, width), jnp.float32)
-        for ref, d in ((rim_left, -1), (rim_right, 1)):
-            @pl.when(jnp.logical_not(there(0, d)))
-            def _():
-                ref[p] = jnp.zeros(ref.shape[1:], jnp.float32)
-        for i in range(4):
-            @pl.when(jnp.logical_not(there(-sides[4 + i][0], -sides[4 + i][1])))
-            def _():
-                for c in range(chunks):
-                    cornered[p, c, i] = jnp.zeros((1, LANES), jnp.float32)
-
     barrier = pltpu.get_barrier_semaphore()
 
     def peers_all():
@@ -296,6 +274,24 @@
             greet(device)
         met = jnp.int32(nx * ny)
 
+    for p in range(2):
+        for r, d in ((0, -1), (rows + 2, 1)):
+            @pl.when(jnp.logical_not(there(d, 0)))
+            def _():
+                field[p, r : r + 2] = jnp.zeros((2, layers + 2 * SUB, width), jnp.float32)
+        for r in range(2, rows + 2):
+            for s in (0, SUB + layers):
+                field[p, r, s : s + SUB] = jnp.zeros((SUB, width), jnp.float32)
+        for ref, d in ((rim_left, -1), (rim_right, 1)):
+            @pl.when(jnp.logical_not(there(0, d)))
+            def _():
+                ref[p] = jnp.zeros(ref.shape[1:], jnp.float32)
+        for i in range(4):
+            @pl.when(jnp.logical_not(there(-sides[4 + i][0], -sides[4 + i][1])))
+            def _():
+                for c in range(chunks):
+                    cornered[p, c, i] = jnp.zeros((1, LANES), jnp.float32)
+
     lane = lax.broadcasted_iota(jnp.int32, (SUB, LANES), 1)
     sub = lax.broadcasted_iota(jnp.int32, (SUB, width), 0)
 
@@ -355,7 +351,6 @@
 
     pl.semaphore_wait(barrier, met)
     lax.fori_loop(0, chunks, first_pass, 0)
-    fetch.wait()
 
     def gather(j, total):
         for t in range(SUB):
@@ -638,7 +633,7 @@
     out_x, out_p, out_r, out_q, out_s = pl.pallas_call(
         functools.partial(kernel, (nx, ny)),
         out_shape=(jax.ShapeDtypeStruct((layers, rows, width), f32),) * 4 + (jax.ShapeDtypeStruct((SUB, width), f32),),
-        in_specs=[pl.BlockSpec(memory_space=pl.ANY)] + [vmem] * 4,
+        in_specs=[vmem] * 5,
         out_specs=(vmem,) * 5,
         scratch_shapes=[
             pltpu.VMEM((2, rows + 4, layers + 2 * SUB, width), f32),
@@ -665,8 +660,6 @@
             dma((nx * ny - 1,)),
             dma((nx * ny - 1,)),
             dma((nx * ny - 1,)),
-            pltpu.VMEM((layers, rows, width), f32),
-            dma,
         ],
         compiler_params=pltpu.CompilerParams(
             collective_id=0, has_side_effects=True, vmem_limit_bytes=40 * 1024 * 1024

time: 60.1 us -> 56.5 us (0.940)
  Pallas kernels: 56.8 us -> 53.2 us
    pallas_call x1, Pallas kernels: 56.8 us -> 53.2 us  [on_device(): pl.pallas_call(functools.partial(kernel, (nx, ny)), out_shape=(jax.ShapeD...]
where the time goes in v3:
time: 56.5 us; the launch traced here: 56.4 us
  Pallas kernels  53.2 us (94%)
  other arithmetic  2.5 us (4%)
  between operations  0.7 us (1%)
    pallas_call x1, Pallas kernels, on_device(): pl.pallas_call(functools.partial(kernel, (nx, ny)), out_shape=(jax.ShapeD...  53.2 us
    transpose x1, other arithmetic, turned(): return jnp.transpose(a[0].astype(jnp.float32), (1, 0, 2))  1.28 us
    broadcast_in_dim x1, other arithmetic, on_device(): return tuple((o[None] for o in (solved, residual)))  1.22 us

profile of v3, /device:TPU:0, one launch (start us, length us, event | category | flops | bytes accessed | tf_op | source)
XLA Modules:
  0.0 56.4 jit_solution(1925867816115655262)
XLA Ops:
  0.6 0.0 copy-start
  0.6 0.0 copy-start.1
  0.7 0.0 copy-start.2
  0.7 1.3 %convert_bitcast_fusion = (f32[8,80,256]{2,1,0:T(8,128)S(1)}, f32[8,80,256]{2,1,0:T(8,128)S(1)}) fusion(bf16[1,80,8,256]{3,2,1,0:T(8,128)(2,1)} %param.7, bf16[1,80,8,256]{3,2,1,0:T(8,128)(2,1)} %param.6), kind=kLoop, calls=%fused_computation | loop fusion | flops 327680 | bytes 1966080 | tf_op jit(solution)/shard_map/transpose | solution.py:624
  1.9 0.0 copy-done
  2.0 0.0 copy-done.1
  2.0 0.0 copy-done.2
  2.0 53.2 %krylov.1 = (f32[80,8,256]{2,1,0:T(8,128)S(1)}, f32[80,8,256]{2,1,0:T(8,128)S(1)}, f32[80,8,256]{2,1,0:T(8,128)S(1)}, f32[80,8,256]{2,1,0:T(8,128)S(1)}, f32[8,256]{1,0:T(8,128)S(1)}) custom-call(f32[80,8,256]{2,1,0:T(8,128)S(1)} %bitcast.16, f32[8,80,256]{2,1,0:T(8,128)S(1)} %get-tuple-element.15.conduct, f32[8,80,256]{2,1,0:T(8,128)S(1)} %get-tuple-element.14.extra, ...), custom_call_target="tpu_custom_call" | custom-call | tf_op jit(solution)/shard_map/krylov/pallas_call | solution.py:633
  55.1 1.2 %subtract_bitcast_fusion = (f32[1,80,8,256]{3,2,1,0:T(8,128)}, f32[1,80,8,256]{3,2,1,0:T(8,128)}) fusion(f32[80,8,256]{2,1,0:T(8,128)S(1)} %get-tuple-element.10, f32[80,8,256]{2,1,0:T(8,128)S(1)} %get-tuple-element.11, f32[256]{0:T(256)S(1)} %bitcast.17, f32[80,8,256]{2,1,0:T(8,128)S(1)} %get-tuple-element.7, f32[80,8,256]{2,1,0:T(8,128)S(1)} %get-tuple-element.9), kind=kLoop, calls=%fused_computation.2 | loop fusion | flops 655360 | bytes 3933184 | tf_op jit(solution)/shard_map/broadcast_in_dim | solution.py:671
  (1 shorter events, 0.0 us)
Async XLA Ops:
  0.6 1.3 %copy-start = (f32[1,80,8,256]{3,2,1,0:T(8,128)S(1)}, f32[1,80,8,256]{3,2,1,0:T(8,128)}, u32[]{:S(2)}) copy-start(f32[1,80,8,256]{3,2,1,0:T(8,128)} %param.5) | copy-start | bytes 1966084
  0.6 1.3 %copy-start.1 = (s32[8,256]{1,0:T(8,128)S(1)}, s32[8,256]{1,0:T(8,128)}, u32[]{:S(2)}) copy-start(s32[8,256]{1,0:T(8,128)} %ice.1) | copy-start | bytes 24580
  0.7 1.3 %copy-start.2 = (s32[8,256]{1,0:T(8,128)S(1)}, s32[8,256]{1,0:T(8,128)}, u32[]{:S(2)}) copy-start(s32[8,256]{1,0:T(8,128)} %grounded.1) | copy-start | bytes 24580

commit v4 on v3

--- a/solution.py
+++ b/solution.py
@@ -120,9 +120,10 @@
     nx, ny = sizes
     rows, layers, width = conduct.shape
     tiles = layers // SUB
-    chunks = corner.shape[1]
+    chunks = send_sem.shape[1]
     per = tiles // chunks
     deep = per * SUB
+    group = 2 if 8 * deep <= LANES else 1
     gg, gx, gy = lax.axis_index("group"), lax.axis_index("gx"), lax.axis_index("gy")
     is_ice = gg == 0
 
@@ -155,12 +156,12 @@
         elif i == 3:
             source, target = pack.at[p, flat], rim_left.at[p, flat]
         else:
-            source, target = corner.at[p, c], cornered.at[p, c, i - 4]
+            source, target = corner.at[p, c // group], cornered.at[p, c // group, i - 4]
         return pltpu.make_async_remote_copy(
             src_ref=source,
             dst_ref=target,
-            send_sem=send_sem.at[p, c, i],
-            recv_sem=recv_sem.at[p, c, i],
+            send_sem=send_sem.at[p, c if i < 4 else c // group * group, i],
+            recv_sem=recv_sem.at[p, c if i < 4 else c // group * group, i],
             device_id=at(dx, dy),
             device_id_type=pl.DeviceIdType.MESH,
         )
@@ -169,8 +170,9 @@
     relayed = gg == 1
     lag = min(3, chunks - 1)
 
-    def each(toward, act):
-        for i, (dx, dy) in enumerate(sides):
+    def each(toward, act, chosen=range(8)):
+        for i in chosen:
+            dx, dy = sides[i]
             ok = there(toward * dx, toward * dy)
             if i < 2 and detours:
                 split = gx == ((2 - i) if toward > 0 else (1 + i))
@@ -217,26 +219,54 @@
                 away(path, p, c, slot).wait_recv()
                 onward(path, p, c, slot).start()
 
-    def start(p, c, slot):
+    def first_of(c):
+        return lax.rem(c, group) == 0
+
+    def last_of(c):
+        return (lax.rem(c, group) == group - 1) | (c == chunks - 1)
+
+    def start_rows(p, c, slot):
         for path in detours:
             @pl.when((gx == path[0]) & relayed)
             def _():
                 away(path, p, c, slot).start()
-        each(1, lambda i, span: copy_of(i, p, c, span).start())
+        for order in ((1, 0), (0, 1)):
+            @pl.when((gx == 2) if order == (0, 1) else (gx != 2))
+            def _():
+                each(1, lambda i, span: copy_of(i, p, c, span).start(), order)
+
+        @pl.when(last_of(c))
+        def _():
+            each(1, lambda i, span: copy_of(i, p, c, span).start(), range(4, 8))
+
+    def start_rest(p, c):
+        each(1, lambda i, span: copy_of(i, p, c, span).start(), range(2, 4))
+
+    def start(p, c, slot):
+        start_rows(p, c, slot)
+        start_rest(p, c)
 
     def finish_recv(p, c):
         for path in detours:
             @pl.when((gx == path[2]) & relayed)
             def _():
                 onward(path, p, c, 0).wait_recv()
-        each(-1, lambda i, span: copy_of(i, p, c, span).wait_recv())
+        each(-1, lambda i, span: copy_of(i, p, c, span).wait_recv(), range(4))
+
+        @pl.when(first_of(c))
+        def _():
+            each(-1, lambda i, span: copy_of(i, p, c, span).wait_recv(), range(4, 8))
 
     def finish_send(p, c):
         for path in detours:
             @pl.when((gx == path[0]) & relayed)
             def _():
                 away(path, p, c, 0).wait_send()
-        each(1, lambda i, span: copy_of(i, p, c, span).wait_send())
+        each(1, lambda i, span: copy_of(i, p, c, span).wait_send(), range(4))
+
+        @pl.when(first_of(c))
+        def _():
+            each(1, lambda i, span: copy_of(i, p, c, span).wait_send(), range(4, 8))
 
     barrier = pltpu.get_barrier_semaphore()
 
@@ -289,7 +319,7 @@
         for i in range(4):
             @pl.when(jnp.logical_not(there(-sides[4 + i][0], -sides[4 + i][1])))
             def _():
-                for c in range(chunks):
+                for c in range(cornered.shape[1]):
                     cornered[p, c, i] = jnp.zeros((1, LANES), jnp.float32)
 
     lane = lax.broadcasted_iota(jnp.int32, (SUB, LANES), 1)
@@ -315,7 +345,17 @@
         return tile, corners
 
     def put_corner(p, c, corners):
-        corner[p, c] = jnp.sum(corners, axis=0, keepdims=True)
+        value = jnp.sum(corners, axis=0, keepdims=True)
+
+        @pl.when(first_of(c))
+        def _():
+            corner[p, c // group] = value
+
+        if group > 1:
+
+            @pl.when(jnp.logical_not(first_of(c)))
+            def _():
+                corner[p, c // group] = corner[p, c // group] + pltpu.roll(value, LANES // 2, 1)
 
     ice_cells = ice[...].astype(jnp.float32)
     ground_cells = grounded[...].astype(jnp.float32)
@@ -329,11 +369,7 @@
     blank = jnp.zeros((SUB, LANES), jnp.float32)
     zero = jnp.zeros((SUB, width), jnp.float32)
 
-    def first_pass(c, carry):
-        @pl.when(c >= lag)
-        def _():
-            forward(c - lag)
-
+    def prepare(c):
         corners = blank
         for t in range(per):
             j = c * per + t
@@ -346,11 +382,22 @@
                 tile, corners = pack_row(x, value, tile, t, corners)
             pack[0, ls, :] = tile
         put_corner(0, c, corners)
-        start(0, c, 0)
+
+    def first_pass(c, carry):
+        start(0, c - 1, 0)
+
+        @pl.when(c > lag)
+        def _():
+            forward(c - 1 - lag)
+
+        prepare(c)
         return carry
 
+    prepare(0)
     pl.semaphore_wait(barrier, met)
-    lax.fori_loop(0, chunks, first_pass, 0)
+    lax.fori_loop(1, chunks, first_pass, 0)
+    start(0, chunks - 1, 0)
+    forward(chunks - 1 - lag)
 
     def gather(j, total):
         for t in range(SUB):
@@ -374,7 +421,10 @@
     )
     to_partner.start()
 
-    def spread_block(p, c, t):
+    outer = tuple(x for x in range(rows) if x < 2 or x >= rows - 2)
+    inner = tuple(x for x in range(rows) if x not in outer)
+
+    def spread_block(p, c, t, xs):
         j = c * per + t
         here = pl.ds(pl.multiple_of(j * SUB + SUB, SUB), SUB)
         below = pl.ds(pl.multiple_of(j * SUB, SUB), SUB)
@@ -382,7 +432,9 @@
         from_right, from_left = rim_right[p, below, :], rim_left[p, below, :]
 
         def column(i):
-            row = jnp.broadcast_to(cornered[p, c, i], (SUB, LANES))
+            row = jnp.broadcast_to(cornered[p, c // group, i], (SUB, LANES))
+            if group > 1:
+                row = jnp.where(first_of(c), row, pltpu.roll(row, LANES // 2, 1))
             return jnp.sum(jnp.where(spot(i, t), row, 0.0), axis=1, keepdims=True)
 
         def rim(x):
@@ -410,9 +462,11 @@
                 out.append(up + down)
             return jnp.concatenate(out, axis=1)
 
-        e = [line(0), line(1)]
-        for x in range(rows):
-            e.append(line(x + 2))
+        e = {}
+        for x in xs:
+            for i in range(x, x + 3):
+                if i not in e:
+                    e[i] = line(i)
             beside = [a + b for a, b in zip(e[x], e[x + 2])]
             h = [a + cross_weight * b for a, b in zip(e[x + 1], beside)]
             mine = field[p, x + 2, here, :]
@@ -439,33 +493,41 @@
     def zeroth(c, acc):
         forward(chunks + c - lag)
         finish_recv(0, c)
-        corners = blank
-        for t in range(per):
-            j = c * per + t
-            ls = pl.ds(pl.multiple_of(j * SUB, SUB), SUB)
-            layer = sub + j * SUB
-            at_edge = layer == edge
-            at_bottom = layer == 0
-            tile = blank
-            for x, around in enumerate(list(spread_block(0, c, t))):
-                own = coupling[x, ls, :]
-                diag = (
-                    extra[x, ls, :] + jnp.where(at_bottom, wide(friction, x), 0.0) + own * around
-                )
-                inverse = 1.0 / diag
-                source = wide(active, x) * force[ls, x, :] + jnp.where(at_edge, wide(term, x), 0.0)
-                vector = inverse * source
-                diagonal[x, ls, :] = diag
-                scaled[x, ls, :] = inverse * own
-                basis[0, x, ls, :] = zero
-                basis[1, x, ls, :] = vector
-                value = own * vector
-                field[1, x + 2, pl.ds(pl.multiple_of(j * SUB + SUB, SUB), SUB), :] = value
-                tile, corners = pack_row(x, value, tile, t, corners)
-                acc = acc + source * vector
-            pack[1, ls, :] = tile
-        put_corner(1, c, corners)
-        start(1, c, 1)
+        corners, packed = blank, [blank] * per
+        for xs in (outer, inner):
+            for t in range(per):
+                j = c * per + t
+                ls = pl.ds(pl.multiple_of(j * SUB, SUB), SUB)
+                layer = sub + j * SUB
+                at_edge = layer == edge
+                at_bottom = layer == 0
+                for x, around in zip(xs, list(spread_block(0, c, t, xs))):
+                    own = coupling[x, ls, :]
+                    diag = (
+                        extra[x, ls, :]
+                        + jnp.where(at_bottom, wide(friction, x), 0.0)
+                        + own * around
+                    )
+                    inverse = 1.0 / diag
+                    source = wide(active, x) * force[ls, x, :] + jnp.where(
+                        at_edge, wide(term, x), 0.0
+                    )
+                    vector = inverse * source
+                    diagonal[x, ls, :] = diag
+                    scaled[x, ls, :] = inverse * own
+                    basis[0, x, ls, :] = zero
+                    basis[1, x, ls, :] = vector
+                    value = own * vector
+                    after = pl.ds(pl.multiple_of(j * SUB + SUB, SUB), SUB)
+                    field[1, x + 2, after, :] = value
+                    packed[t], corners = pack_row(x, value, packed[t], t, corners)
+                    acc = acc + source * vector
+                if xs is inner:
+                    pack[1, ls, :] = packed[t]
+            if xs is outer:
+                put_corner(1, c, corners)
+                start_rows(1, c, 1)
+        start_rest(1, c)
         return acc
 
     partial[0] = fold(lax.fori_loop(0, chunks, zeroth, zero))
@@ -524,31 +586,37 @@
 
             finish_recv(p, c)
             finish_send(q, c)
-            corners = blank
-            for t in range(per):
-                j = c * per + t
-                ls = pl.ds(pl.multiple_of(j * SUB, SUB), SUB)
-                tile = blank
-                vectors, values = [], []
-                for x, around in enumerate(list(spread_block(p, c, t))):
-                    vector = gain * (scaled[x, ls, :] * around) - basis[k - 1, x, ls, :]
-                    weighted = diagonal[x, ls, :] * vector
-                    value = coupling[x, ls, :] * vector
-                    own_acc = own_acc + weighted * vector
-                    cross_acc = cross_acc + weighted * basis[k, x, ls, :]
-                    tile, corners = pack_row(x, value, tile, t, corners)
-                    vectors.append(vector)
-                    values.append(value)
-                after = pl.ds(pl.multiple_of(j * SUB + SUB, SUB), SUB)
-                for x in range(rows):
-                    basis[k + 1, x, ls, :] = vectors[x]
-                    field[q, x + 2, after, :] = values[x]
-                pack[q, ls, :] = tile
-            put_corner(q, c, corners)
+            corners, packed = blank, [blank] * per
+            for xs in (outer, inner):
+                for t in range(per):
+                    j = c * per + t
+                    ls = pl.ds(pl.multiple_of(j * SUB, SUB), SUB)
+                    vectors, values = [], []
+                    for x, around in zip(xs, list(spread_block(p, c, t, xs))):
+                        vector = gain * (scaled[x, ls, :] * around) - basis[k - 1, x, ls, :]
+                        weighted = diagonal[x, ls, :] * vector
+                        value = coupling[x, ls, :] * vector
+                        own_acc = own_acc + weighted * vector
+                        cross_acc = cross_acc + weighted * basis[k, x, ls, :]
+                        packed[t], corners = pack_row(x, value, packed[t], t, corners)
+                        vectors.append(vector)
+                        values.append(value)
+                    after = pl.ds(pl.multiple_of(j * SUB + SUB, SUB), SUB)
+                    for x, vector, value in zip(xs, vectors, values):
+                        basis[k + 1, x, ls, :] = vector
+                        field[q, x + 2, after, :] = value
+                    if xs is inner:
+                        pack[q, ls, :] = packed[t]
+                if xs is outer:
+                    put_corner(q, c, corners)
+
+                    @pl.when(k < ITERS)
+                    def _():
+                        start_rows(q, c, k + 1)
 
             @pl.when(k < ITERS)
             def _():
-                start(q, c, k + 1)
+                start_rest(q, c)
 
             return own_acc, cross_acc
 
@@ -626,6 +694,8 @@
     _, layers, rows, width = forcing.shape
     tiles = layers // SUB
     chunks = tiles // next(t for t in CHUNK_TILES if tiles % t == 0)
+    pairs = 2 if 8 * (layers // chunks) <= LANES else 1
+    rows_of_corners = -(-chunks // pairs)
     f32 = jnp.float32
     block = jax.ShapeDtypeStruct((rows, layers, width), f32)
     vmem = pl.BlockSpec(memory_space=pltpu.VMEM)
@@ -640,8 +710,8 @@
             pltpu.VMEM((2, layers, LANES), f32),
             pltpu.VMEM((2, layers, LANES), f32),
             pltpu.VMEM((2, layers, LANES), f32),
-            pltpu.VMEM((2, chunks, 1, LANES), f32),
-            pltpu.VMEM((2, chunks, 4, 1, LANES), f32),
+            pltpu.VMEM((2, rows_of_corners, 1, LANES), f32),
+            pltpu.VMEM((2, rows_of_corners, 4, 1, LANES), f32),
             pltpu.VMEM((ITERS + 1, 2, layers, width), f32),
             pltpu.VMEM((ITERS + 2, rows, layers, width), f32),
             pltpu.VMEM((rows, layers, width), f32),

time: 56.5 us -> 55.7 us (0.986)
  Pallas kernels: 53.2 us -> 52.3 us
    pallas_call x1, Pallas kernels: 53.2 us -> 52.3 us  [on_device(): pl.pallas_call(functools.partial(kernel, (nx, ny)), out_shape=(jax.ShapeD...]
where the time goes in v4:
time: 55.7 us; the launch traced here: 55.5 us
  Pallas kernels  52.3 us (94%)
  other arithmetic  2.5 us (4%)
  between operations  0.7 us (1%)
    pallas_call x1, Pallas kernels, on_device(): pl.pallas_call(functools.partial(kernel, (nx, ny)), out_shape=(jax.ShapeD...  52.3 us
    transpose x1, other arithmetic, turned(): return jnp.transpose(a[0].astype(jnp.float32), (1, 0, 2))  1.28 us
    broadcast_in_dim x1, other arithmetic, on_device(): return tuple((o[None] for o in (solved, residual)))  1.22 us

profile of v4, /device:TPU:0, one launch (start us, length us, event | category | flops | bytes accessed | tf_op | source)
XLA Modules:
  0.0 55.5 jit_solution(18389011096301513852)
XLA Ops:
  0.6 0.0 copy-start
  0.6 0.0 copy-start.1
  0.7 0.0 copy-start.2
  0.7 1.3 %convert_bitcast_fusion = (f32[8,80,256]{2,1,0:T(8,128)S(1)}, f32[8,80,256]{2,1,0:T(8,128)S(1)}) fusion(bf16[1,80,8,256]{3,2,1,0:T(8,128)(2,1)} %param.7, bf16[1,80,8,256]{3,2,1,0:T(8,128)(2,1)} %param.6), kind=kLoop, calls=%fused_computation | loop fusion | flops 327680 | bytes 1966080 | tf_op jit(solution)/shard_map/transpose | solution.py:692
  1.9 0.0 copy-done
  2.0 0.0 copy-done.1
  2.0 0.0 copy-done.2
  2.0 52.3 %krylov.1 = (f32[80,8,256]{2,1,0:T(8,128)S(1)}, f32[80,8,256]{2,1,0:T(8,128)S(1)}, f32[80,8,256]{2,1,0:T(8,128)S(1)}, f32[80,8,256]{2,1,0:T(8,128)S(1)}, f32[8,256]{1,0:T(8,128)S(1)}) custom-call(f32[80,8,256]{2,1,0:T(8,128)S(1)} %bitcast.16, f32[8,80,256]{2,1,0:T(8,128)S(1)} %get-tuple-element.15.conduct, f32[8,80,256]{2,1,0:T(8,128)S(1)} %get-tuple-element.14.extra, ...), custom_call_target="tpu_custom_call" | custom-call | tf_op jit(solution)/shard_map/krylov/pallas_call | solution.py:703
  54.3 1.2 %subtract_bitcast_fusion = (f32[1,80,8,256]{3,2,1,0:T(8,128)}, f32[1,80,8,256]{3,2,1,0:T(8,128)}) fusion(f32[80,8,256]{2,1,0:T(8,128)S(1)} %get-tuple-element.10, f32[80,8,256]{2,1,0:T(8,128)S(1)} %get-tuple-element.11, f32[256]{0:T(256)S(1)} %bitcast.17, f32[80,8,256]{2,1,0:T(8,128)S(1)} %get-tuple-element.7, f32[80,8,256]{2,1,0:T(8,128)S(1)} %get-tuple-element.9), kind=kLoop, calls=%fused_computation.2 | loop fusion | flops 655360 | bytes 3933184 | tf_op jit(solution)/shard_map/broadcast_in_dim | solution.py:741
  (1 shorter events, 0.0 us)
Async XLA Ops:
  0.6 1.3 %copy-start = (f32[1,80,8,256]{3,2,1,0:T(8,128)S(1)}, f32[1,80,8,256]{3,2,1,0:T(8,128)}, u32[]{:S(2)}) copy-start(f32[1,80,8,256]{3,2,1,0:T(8,128)} %param.5) | copy-start | bytes 1966084
  0.6 1.3 %copy-start.1 = (s32[8,256]{1,0:T(8,128)S(1)}, s32[8,256]{1,0:T(8,128)}, u32[]{:S(2)}) copy-start(s32[8,256]{1,0:T(8,128)} %ice.1) | copy-start | bytes 24580
  0.7 1.3 %copy-start.2 = (s32[8,256]{1,0:T(8,128)S(1)}, s32[8,256]{1,0:T(8,128)}, u32[]{:S(2)}) copy-start(s32[8,256]{1,0:T(8,128)} %grounded.1) | copy-start | bytes 24580

commit v5 on v4

--- a/solution.py
+++ b/solution.py
@@ -84,9 +84,9 @@
     sizes,
     force,
     conduct,
-    extra,
-    ice,
-    grounded,
+    extra_half,
+    active_cells,
+    friction_cells,
     out_x,
     out_p,
     out_r,
@@ -116,9 +116,10 @@
     se_recv,
     sa_send,
     sa_recv,
+    extra,
 ):
     nx, ny = sizes
-    rows, layers, width = conduct.shape
+    layers, rows, width = conduct.shape
     tiles = layers // SUB
     chunks = send_sem.shape[1]
     per = tiles // chunks
@@ -246,16 +247,23 @@
         start_rows(p, c, slot)
         start_rest(p, c)
 
-    def finish_recv(p, c):
+    def finish_rows(p, c):
         for path in detours:
             @pl.when((gx == path[2]) & relayed)
             def _():
                 onward(path, p, c, 0).wait_recv()
-        each(-1, lambda i, span: copy_of(i, p, c, span).wait_recv(), range(4))
+        each(-1, lambda i, span: copy_of(i, p, c, span).wait_recv(), range(2))
 
         @pl.when(first_of(c))
         def _():
             each(-1, lambda i, span: copy_of(i, p, c, span).wait_recv(), range(4, 8))
+
+    def finish_columns(p, c):
+        each(-1, lambda i, span: copy_of(i, p, c, span).wait_recv(), range(2, 4))
+
+    def finish_recv(p, c):
+        finish_columns(p, c)
+        finish_rows(p, c)
 
     def finish_send(p, c):
         for path in detours:
@@ -357,11 +365,7 @@
             def _():
                 corner[p, c // group] = corner[p, c // group] + pltpu.roll(value, LANES // 2, 1)
 
-    ice_cells = ice[...].astype(jnp.float32)
-    ground_cells = grounded[...].astype(jnp.float32)
-    ocean = jnp.where(is_ice, 0.0, 1.0).astype(jnp.float32)
-    active = ice_cells * (1.0 - ocean * ground_cells)
-    friction = (1.0 - ocean) * friction_gain * ground_cells * ice_cells
+    active, friction = active_cells[...], friction_cells[...]
 
     def wide(array, x):
         return jnp.broadcast_to(array[x : x + 1, :], (SUB, width))
@@ -376,7 +380,7 @@
             ls = pl.ds(pl.multiple_of(j * SUB, SUB), SUB)
             tile = blank
             for x in range(rows):
-                value = jnp.sqrt(conduct[x, ls, :]) * wide(active, x)
+                value = jnp.sqrt(conduct[ls, x, :]) * wide(active, x)
                 coupling[x, ls, :] = value
                 field[0, x + 2, pl.ds(pl.multiple_of(j * SUB + SUB, SUB), SUB), :] = value
                 tile, corners = pack_row(x, value, tile, t, corners)
@@ -401,6 +405,7 @@
 
     def gather(j, total):
         for t in range(SUB):
+            extra[j * SUB + t] = extra_half[j * SUB + t].astype(jnp.float32)
             total = total + force[j * SUB + t]
         return total
 
@@ -504,7 +509,7 @@
                 for x, around in zip(xs, list(spread_block(0, c, t, xs))):
                     own = coupling[x, ls, :]
                     diag = (
-                        extra[x, ls, :]
+                        extra[ls, x, :]
                         + jnp.where(at_bottom, wide(friction, x), 0.0)
                         + own * around
                     )
@@ -578,12 +583,7 @@
 
         def block(c, accs):
             own_acc, cross_acc = accs
-            message = (k + 1) * chunks + c - lag
-
-            @pl.when(message < (ITERS + 1) * chunks)
-            def _():
-                forward(message)
-
+            forward((k + 1) * chunks + c - lag)
             finish_recv(p, c)
             finish_send(q, c)
             corners, packed = blank, [blank] * per
@@ -610,34 +610,49 @@
                 if xs is outer:
                     put_corner(q, c, corners)
 
-                    @pl.when(k < ITERS)
-                    def _():
-                        start_rows(q, c, k + 1)
-
-            @pl.when(k < ITERS)
-            def _():
-                start_rest(q, c)
-
+                    start_rows(q, c, k + 1)
+
+            start_rest(q, c)
             return own_acc, cross_acc
 
         own_acc, cross_acc = lax.fori_loop(0, chunks, block, (zero, zero))
         partial[2 * k] = fold(own_acc)
         partial[2 * k + 1] = fold(cross_acc)
 
-        @pl.when(k == ITERS - 1)
+        return carry
+
+    lax.fori_loop(1, ITERS, step, 0)
+    early_start()
+    now = ITERS % 2
+
+    def final_rows(c, acc, xs):
+        for t in range(per):
+            ls = pl.ds(pl.multiple_of((c * per + t) * SUB, SUB), SUB)
+            for x, around in zip(xs, list(spread_block(now, c, t, xs))):
+                vector = 2.0 * (scaled[x, ls, :] * around) - basis[ITERS - 1, x, ls, :]
+                acc = acc + diagonal[x, ls, :] * vector * basis[ITERS, x, ls, :]
+                basis[ITERS + 1, x, ls, :] = vector
+        return acc
+
+    def final_block(c, acc):
+        @pl.when(c < lag)
         def _():
-            early_start()
-
-        return carry
-
-    lax.fori_loop(1, ITERS + 1, step, 0)
-    sum_all[gx * ny + gy] = jnp.sum(partial[2 * ITERS + 1], axis=0, keepdims=True)
+            forward((ITERS + 1) * chunks + c - lag)
+
+        finish_columns(now, c)
+        acc = final_rows(c, acc, inner)
+        finish_rows(now, c)
+        return final_rows(c, acc, outer)
+
+    acc = fold(lax.fori_loop(0, chunks, final_block, zero))
+    sum_all[gx * ny + gy] = jnp.sum(acc, axis=0, keepdims=True)
     to_all = copies(sum_all, gx * ny + gy, peers_all(), sa_send, sa_recv)
     for copy in to_all:
         copy.start()
 
     def settle(c, carry):
-        finish_send(ITERS % 2, c)
+        finish_send(1 - now, c)
+        finish_send(now, c)
         for path in detours:
             @pl.when((gx == path[1]) & relayed)
             def _():
@@ -688,9 +703,14 @@
 
 
 def on_device(nx, ny, forcing, conduct, diag_add, ice_mask, grounded):
-    def turned(a):
-        return jnp.transpose(a[0].astype(jnp.float32), (1, 0, 2))
-
+    wide_conduct = conduct[0].astype(jnp.float32)
+    wide_conduct, ice_mask, grounded = lax.optimization_barrier(
+        (wide_conduct, ice_mask, grounded)
+    )
+    ice_cells, ground_cells = ice_mask.astype(jnp.float32), grounded.astype(jnp.float32)
+    ocean = jnp.where(lax.axis_index("group") == 0, 0.0, 1.0)
+    active = ice_cells * (1.0 - ocean * ground_cells)
+    friction = (1.0 - ocean) * friction_gain * ground_cells * ice_cells
     _, layers, rows, width = forcing.shape
     tiles = layers // SUB
     chunks = tiles // next(t for t in CHUNK_TILES if tiles % t == 0)
@@ -719,7 +739,7 @@
             pltpu.VMEM((rows, layers, width), f32),
             pltpu.VMEM((2, rows, width), f32),
             pltpu.VMEM((2, rows, width), f32),
-            pltpu.VMEM((2 * ITERS + 2, SUB, LANES), f32),
+            pltpu.VMEM((2 * ITERS, SUB, LANES), f32),
             pltpu.VMEM((nx * ny, 1, LANES), f32),
             pltpu.VMEM((nx * ny, 1, LANES), f32),
             dma((2, chunks, 8)),
@@ -730,12 +750,13 @@
             dma((nx * ny - 1,)),
             dma((nx * ny - 1,)),
             dma((nx * ny - 1,)),
+            pltpu.VMEM((layers, rows, width), f32),
         ],
         compiler_params=pltpu.CompilerParams(
             collective_id=0, has_side_effects=True, vmem_limit_bytes=40 * 1024 * 1024
         ),
         name="krylov",
-    )(forcing[0], turned(conduct), turned(diag_add), ice_mask, grounded)
+    )(forcing[0], wide_conduct, diag_add[0], active, friction)
     step = out_s[:1]
     solved, residual = out_x + step * out_p, out_r - step * out_q
     return tuple(o[None] for o in (solved, residual))

time: 55.7 us -> 55.1 us (0.989)
    transpose x1 -> x0, other arithmetic: 1.28 us -> none  [turned(): return jnp.transpose(a[0].astype(jnp.float32), (1, 0, 2))]
    convert_element_type x0 -> x1, other arithmetic: none -> 1.09 us  [on_device(): wide_conduct = conduct[0].astype(jnp.float32)]
where the time goes in v5:
time: 55.1 us; the launch traced here: 55 us
  Pallas kernels  51.8 us (94%)
  other arithmetic  2.32 us (4%)
  between operations  0.72 us (1%)
    pallas_call x1, Pallas kernels, on_device(): pl.pallas_call(functools.partial(kernel, (nx, ny)), out_shape=(jax.ShapeD...  51.8 us
    broadcast_in_dim x1, other arithmetic, on_device(): return tuple((o[None] for o in (solved, residual)))  1.22 us

profile of v5, /device:TPU:0, one launch (start us, length us, event | category | flops | bytes accessed | tf_op | source)
XLA Modules:
  0.0 55.0 jit_solution(17829840203437106552)
XLA Ops:
  0.6 0.0 copy-start
  0.7 0.0 copy-start.2
  0.7 0.0 copy-start.3
  0.7 0.0 copy-start.1
  0.7 1.1 %bitcast_convert_fusion.conduct = f32[80,8,256]{2,1,0:T(8,128)S(1)} fusion(bf16[1,80,8,256]{3,2,1,0:T(8,128)(2,1)} %param.6), kind=kLoop, calls=%fused_computation.2 | loop fusion | flops 163840 | bytes 983040 | tf_op jit(solution)/shard_map/convert_element_type | solution.py:706
  1.8 0.0 copy-done.2
  1.8 0.0 copy-done.3
  1.8 0.0 copy-done
  1.8 0.1 copy-done.1
  1.9 51.8 %krylov.1 = (f32[80,8,256]{2,1,0:T(8,128)S(1)}, f32[80,8,256]{2,1,0:T(8,128)S(1)}, f32[80,8,256]{2,1,0:T(8,128)S(1)}, f32[80,8,256]{2,1,0:T(8,128)S(1)}, f32[8,256]{1,0:T(8,128)S(1)}) custom-call(f32[80,8,256]{2,1,0:T(8,128)S(1)} %bitcast.10, f32[80,8,256]{2,1,0:T(8,128)S(1)} %bitcast_convert_fusion.conduct, bf16[80,8,256]{2,1,0:T(8,128)(2,1)S(1)} %bitcast.11, ...), custom_call_target="tpu_custom_call" | custom-call | tf_op jit(solution)/shard_map/krylov/pallas_call | solution.py:723
  53.7 1.2 %subtract_bitcast_fusion = (f32[1,80,8,256]{3,2,1,0:T(8,128)}, f32[1,80,8,256]{3,2,1,0:T(8,128)}) fusion(f32[80,8,256]{2,1,0:T(8,128)S(1)} %get-tuple-element.16, f32[80,8,256]{2,1,0:T(8,128)S(1)} %get-tuple-element.17, f32[256]{0:T(256)S(1)} %bitcast.12, f32[80,8,256]{2,1,0:T(8,128)S(1)} %get-tuple-element.13, f32[80,8,256]{2,1,0:T(8,128)S(1)} %get-tuple-element.15), kind=kLoop, calls=%fused_computation | loop fusion | flops 655360 | bytes 3933184 | tf_op jit(solution)/shard_map/broadcast_in_dim | solution.py:762
  (2 shorter events, 0.0 us)
Async XLA Ops:
  0.6 1.2 %copy-start = (f32[1,80,8,256]{3,2,1,0:T(8,128)S(1)}, f32[1,80,8,256]{3,2,1,0:T(8,128)}, u32[]{:S(2)}) copy-start(f32[1,80,8,256]{3,2,1,0:T(8,128)} %param.5) | copy-start | bytes 1966084
  0.7 1.1 %copy-start.2 = (s32[8,256]{1,0:T(8,128)S(1)}, s32[8,256]{1,0:T(8,128)}, u32[]{:S(2)}) copy-start(s32[8,256]{1,0:T(8,128)} %param.9) | copy-start | bytes 24580
  0.7 1.1 %copy-start.3 = (s32[8,256]{1,0:T(8,128)S(1)}, s32[8,256]{1,0:T(8,128)}, u32[]{:S(2)}) copy-start(s32[8,256]{1,0:T(8,128)} %param.8) | copy-start | bytes 24580
  0.7 1.3 %copy-start.1 = (bf16[1,80,8,256]{3,2,1,0:T(8,128)(2,1)S(1)}, bf16[1,80,8,256]{3,2,1,0:T(8,128)(2,1)}, u32[]{:S(2)}) copy-start(bf16[1,80,8,256]{3,2,1,0:T(8,128)(2,1)} %param.7) | copy-start | bytes 983044

commit v6 on v5

--- a/solution.py
+++ b/solution.py
@@ -312,24 +312,6 @@
             greet(device)
         met = jnp.int32(nx * ny)
 
-    for p in range(2):
-        for r, d in ((0, -1), (rows + 2, 1)):
-            @pl.when(jnp.logical_not(there(d, 0)))
-            def _():
-                field[p, r : r + 2] = jnp.zeros((2, layers + 2 * SUB, width), jnp.float32)
-        for r in range(2, rows + 2):
-            for s in (0, SUB + layers):
-                field[p, r, s : s + SUB] = jnp.zeros((SUB, width), jnp.float32)
-        for ref, d in ((rim_left, -1), (rim_right, 1)):
-            @pl.when(jnp.logical_not(there(0, d)))
-            def _():
-                ref[p] = jnp.zeros(ref.shape[1:], jnp.float32)
-        for i in range(4):
-            @pl.when(jnp.logical_not(there(-sides[4 + i][0], -sides[4 + i][1])))
-            def _():
-                for c in range(cornered.shape[1]):
-                    cornered[p, c, i] = jnp.zeros((1, LANES), jnp.float32)
-
     lane = lax.broadcasted_iota(jnp.int32, (SUB, LANES), 1)
     sub = lax.broadcasted_iota(jnp.int32, (SUB, width), 0)
 
@@ -402,6 +384,24 @@
     lax.fori_loop(1, chunks, first_pass, 0)
     start(0, chunks - 1, 0)
     forward(chunks - 1 - lag)
+
+    for p in range(2):
+        for r, d in ((0, -1), (rows + 2, 1)):
+            @pl.when(jnp.logical_not(there(d, 0)))
+            def _():
+                field[p, r : r + 2] = jnp.zeros((2, layers + 2 * SUB, width), jnp.float32)
+        for r in range(2, rows + 2):
+            for s in (0, SUB + layers):
+                field[p, r, s : s + SUB] = jnp.zeros((SUB, width), jnp.float32)
+        for ref, d in ((rim_left, -1), (rim_right, 1)):
+            @pl.when(jnp.logical_not(there(0, d)))
+            def _():
+                ref[p] = jnp.zeros(ref.shape[1:], jnp.float32)
+        for i in range(4):
+            @pl.when(jnp.logical_not(there(-sides[4 + i][0], -sides[4 + i][1])))
+            def _():
+                for c in range(cornered.shape[1]):
+                    cornered[p, c, i] = jnp.zeros((1, LANES), jnp.float32)
 
     def gather(j, total):
         for t in range(SUB):
@@ -533,6 +533,7 @@
                 put_corner(1, c, corners)
                 start_rows(1, c, 1)
         start_rest(1, c)
+        finish_send(0, c)
         return acc
 
     partial[0] = fold(lax.fori_loop(0, chunks, zeroth, zero))
@@ -585,7 +586,6 @@
             own_acc, cross_acc = accs
             forward((k + 1) * chunks + c - lag)
             finish_recv(p, c)
-            finish_send(q, c)
             corners, packed = blank, [blank] * per
             for xs in (outer, inner):
                 for t in range(per):
@@ -613,6 +613,7 @@
                     start_rows(q, c, k + 1)
 
             start_rest(q, c)
+            finish_send(p, c)
             return own_acc, cross_acc
 
         own_acc, cross_acc = lax.fori_loop(0, chunks, block, (zero, zero))
@@ -651,7 +652,6 @@
         copy.start()
 
     def settle(c, carry):
-        finish_send(1 - now, c)
         finish_send(now, c)
         for path in detours:
             @pl.when((gx == path[1]) & relayed)

time: 55.1 us -> 55.2 us (level)
  no operation moved by 1% of the time
where the time goes in v6:
time: 55.2 us; the launch traced here: 54.9 us
  Pallas kernels  51.7 us (94%)
  other arithmetic  2.32 us (4%)
  between operations  0.72 us (1%)
    pallas_call x1, Pallas kernels, on_device(): pl.pallas_call(functools.partial(kernel, (nx, ny)), out_shape=(jax.ShapeD...  51.7 us
    broadcast_in_dim x1, other arithmetic, on_device(): return tuple((o[None] for o in (solved, residual)))  1.22 us

profile of v6, /device:TPU:0, one launch (start us, length us, event | category | flops | bytes accessed | tf_op | source)
XLA Modules:
  0.0 54.9 jit_solution(4302469008976136714)
XLA Ops:
  0.6 0.0 copy-start
  0.7 0.0 copy-start.2
  0.7 0.0 copy-start.3
  0.7 0.0 copy-start.1
  0.7 1.1 %bitcast_convert_fusion.conduct = f32[80,8,256]{2,1,0:T(8,128)S(1)} fusion(bf16[1,80,8,256]{3,2,1,0:T(8,128)(2,1)} %param.6), kind=kLoop, calls=%fused_computation.2 | loop fusion | flops 163840 | bytes 983040 | tf_op jit(solution)/shard_map/convert_element_type | solution.py:706
  1.8 0.0 copy-done.2
  1.8 0.0 copy-done.3
  1.8 0.0 copy-done
  1.8 0.1 copy-done.1
  1.9 51.7 %krylov.1 = (f32[80,8,256]{2,1,0:T(8,128)S(1)}, f32[80,8,256]{2,1,0:T(8,128)S(1)}, f32[80,8,256]{2,1,0:T(8,128)S(1)}, f32[80,8,256]{2,1,0:T(8,128)S(1)}, f32[8,256]{1,0:T(8,128)S(1)}) custom-call(f32[80,8,256]{2,1,0:T(8,128)S(1)} %bitcast.10, f32[80,8,256]{2,1,0:T(8,128)S(1)} %bitcast_convert_fusion.conduct, bf16[80,8,256]{2,1,0:T(8,128)(2,1)S(1)} %bitcast.11, ...), custom_call_target="tpu_custom_call" | custom-call | tf_op jit(solution)/shard_map/krylov/pallas_call | solution.py:723
  53.7 1.2 %subtract_bitcast_fusion = (f32[1,80,8,256]{3,2,1,0:T(8,128)}, f32[1,80,8,256]{3,2,1,0:T(8,128)}) fusion(f32[80,8,256]{2,1,0:T(8,128)S(1)} %get-tuple-element.16, f32[80,8,256]{2,1,0:T(8,128)S(1)} %get-tuple-element.17, f32[256]{0:T(256)S(1)} %bitcast.12, f32[80,8,256]{2,1,0:T(8,128)S(1)} %get-tuple-element.13, f32[80,8,256]{2,1,0:T(8,128)S(1)} %get-tuple-element.15), kind=kLoop, calls=%fused_computation | loop fusion | flops 655360 | bytes 3933184 | tf_op jit(solution)/shard_map/broadcast_in_dim | solution.py:762
  (2 shorter events, 0.0 us)
Async XLA Ops:
  0.6 1.2 %copy-start = (f32[1,80,8,256]{3,2,1,0:T(8,128)S(1)}, f32[1,80,8,256]{3,2,1,0:T(8,128)}, u32[]{:S(2)}) copy-start(f32[1,80,8,256]{3,2,1,0:T(8,128)} %param.5) | copy-start | bytes 1966084
  0.7 1.1 %copy-start.2 = (s32[8,256]{1,0:T(8,128)S(1)}, s32[8,256]{1,0:T(8,128)}, u32[]{:S(2)}) copy-start(s32[8,256]{1,0:T(8,128)} %param.9) | copy-start | bytes 24580
  0.7 1.1 %copy-start.3 = (s32[8,256]{1,0:T(8,128)S(1)}, s32[8,256]{1,0:T(8,128)}, u32[]{:S(2)}) copy-start(s32[8,256]{1,0:T(8,128)} %param.8) | copy-start | bytes 24580
  0.7 1.3 %copy-start.1 = (bf16[1,80,8,256]{3,2,1,0:T(8,128)(2,1)S(1)}, bf16[1,80,8,256]{3,2,1,0:T(8,128)(2,1)}, u32[]{:S(2)}) copy-start(bf16[1,80,8,256]{3,2,1,0:T(8,128)(2,1)} %param.7) | copy-start | bytes 983044

commit v7 on v6

--- a/solution.py
+++ b/solution.py
@@ -281,7 +281,8 @@
     def peers_all():
         me = gx * ny + gy
         out = []
-        for o in range(1, nx * ny):
+        middle = nx * ny // 2
+        for o in sorted(range(1, nx * ny), key=lambda o: abs(o - middle)):
             peer = lax.rem(me + o, nx * ny)
             out.append((gg, peer // ny, lax.rem(peer, ny)))
         return out
@@ -556,7 +557,11 @@
         ]
 
     def row_of(slots):
-        return functools.reduce(lambda s, t: s + t, [slots[o] for o in range(slots.shape[0])])
+        terms = [slots[o] for o in range(slots.shape[0])]
+        while len(terms) > 1:
+            pairs = [a + b for a, b in zip(terms[::2], terms[1::2])]
+            terms = pairs + terms[len(pairs) * 2 :]
+        return terms[0]
 
     def copies_early():
         return copies(sum_early, gx * ny + gy, peers_all(), se_send, se_recv)
@@ -694,12 +699,12 @@
     lax.fori_loop(0, tiles, last, 0)
 
     for copy in to_all:
+        copy.wait_send()
+    for copy in to_all:
         copy.wait_recv()
     cross = jnp.sum(row_of(sum_all), axis=1, keepdims=True)
     cross = jnp.broadcast_to(cross, (SUB, LANES))
     out_s[...] = widen(norm / (fixed + slope * (2.0 * cross - moments[1])))
-    for copy in to_all:
-        copy.wait_send()
 
 
 def on_device(nx, ny, forcing, conduct, diag_add, ice_mask, grounded):

time: 55.2 us -> 55.4 us (level)
  no operation moved by 1% of the time
where the time goes in v7:
time: 55.4 us; the launch traced here: 54.9 us
  Pallas kernels  51.7 us (93%)
  other arithmetic  2.32 us (4%)
  between operations  0.72 us (1%)
    pallas_call x1, Pallas kernels, on_device(): pl.pallas_call(functools.partial(kernel, (nx, ny)), out_shape=(jax.ShapeD...  51.7 us
    broadcast_in_dim x1, other arithmetic, on_device(): return tuple((o[None] for o in (solved, residual)))  1.22 us

profile of v7, /device:TPU:0, one launch (start us, length us, event | category | flops | bytes accessed | tf_op | source)
XLA Modules:
  0.0 54.9 jit_solution(13757754693492273965)
XLA Ops:
  0.6 0.0 copy-start
  0.7 0.0 copy-start.2
  0.7 0.0 copy-start.3
  0.7 0.0 copy-start.1
  0.7 1.1 %bitcast_convert_fusion.conduct = f32[80,8,256]{2,1,0:T(8,128)S(1)} fusion(bf16[1,80,8,256]{3,2,1,0:T(8,128)(2,1)} %param.6), kind=kLoop, calls=%fused_computation.2 | loop fusion | flops 163840 | bytes 983040 | tf_op jit(solution)/shard_map/convert_element_type | solution.py:711
  1.8 0.0 copy-done.2
  1.8 0.0 copy-done.3
  1.8 0.0 copy-done
  1.8 0.1 copy-done.1
  1.9 51.7 %krylov.1 = (f32[80,8,256]{2,1,0:T(8,128)S(1)}, f32[80,8,256]{2,1,0:T(8,128)S(1)}, f32[80,8,256]{2,1,0:T(8,128)S(1)}, f32[80,8,256]{2,1,0:T(8,128)S(1)}, f32[8,256]{1,0:T(8,128)S(1)}) custom-call(f32[80,8,256]{2,1,0:T(8,128)S(1)} %bitcast.10, f32[80,8,256]{2,1,0:T(8,128)S(1)} %bitcast_convert_fusion.conduct, bf16[80,8,256]{2,1,0:T(8,128)(2,1)S(1)} %bitcast.11, ...), custom_call_target="tpu_custom_call" | custom-call | tf_op jit(solution)/shard_map/krylov/pallas_call | solution.py:728
  53.7 1.2 %subtract_bitcast_fusion = (f32[1,80,8,256]{3,2,1,0:T(8,128)}, f32[1,80,8,256]{3,2,1,0:T(8,128)}) fusion(f32[80,8,256]{2,1,0:T(8,128)S(1)} %get-tuple-element.16, f32[80,8,256]{2,1,0:T(8,128)S(1)} %get-tuple-element.17, f32[256]{0:T(256)S(1)} %bitcast.12, f32[80,8,256]{2,1,0:T(8,128)S(1)} %get-tuple-element.13, f32[80,8,256]{2,1,0:T(8,128)S(1)} %get-tuple-element.15), kind=kLoop, calls=%fused_computation | loop fusion | flops 655360 | bytes 3933184 | tf_op jit(solution)/shard_map/broadcast_in_dim | solution.py:767
  (2 shorter events, 0.0 us)
Async XLA Ops:
  0.6 1.2 %copy-start = (f32[1,80,8,256]{3,2,1,0:T(8,128)S(1)}, f32[1,80,8,256]{3,2,1,0:T(8,128)}, u32[]{:S(2)}) copy-start(f32[1,80,8,256]{3,2,1,0:T(8,128)} %param.5) | copy-start | bytes 1966084
  0.7 1.1 %copy-start.2 = (s32[8,256]{1,0:T(8,128)S(1)}, s32[8,256]{1,0:T(8,128)}, u32[]{:S(2)}) copy-start(s32[8,256]{1,0:T(8,128)} %param.9) | copy-start | bytes 24580
  0.7 1.1 %copy-start.3 = (s32[8,256]{1,0:T(8,128)S(1)}, s32[8,256]{1,0:T(8,128)}, u32[]{:S(2)}) copy-start(s32[8,256]{1,0:T(8,128)} %param.8) | copy-start | bytes 24580
  0.7 1.3 %copy-start.1 = (bf16[1,80,8,256]{3,2,1,0:T(8,128)(2,1)S(1)}, bf16[1,80,8,256]{3,2,1,0:T(8,128)(2,1)}, u32[]{:S(2)}) copy-start(bf16[1,80,8,256]{3,2,1,0:T(8,128)(2,1)} %param.7) | copy-start | bytes 983044
